TPU v7x, 64 devices: a 2x2x8 block of a 4x4x8 slice. The times are simulated.
64 devices in a mesh: dp: 4 (over x, y), sp: 16 (over z, core).
Axes of the slice: x: 2, y: 2, z: 8, core: 2. Of those that a mesh axis runs over, the one named last changes fastest.
The devices are a block of a 4x4x8 slice.
Arguments:
- x: bfloat16 [24576, 2048], P(('dp', 'sp')), parts along dimension 0
- wq: bfloat16 [2048, 2048], replicated
- wk: bfloat16 [2048, 2048], replicated
- wv: bfloat16 [2048, 2048], replicated
- wo: bfloat16 [2048, 2048], replicated
- idx: int32 [24576, 6], P(('dp', 'sp')), parts along dimension 0
- probs: float32 [24576, 64], P(('dp', 'sp')), parts along dimension 0
Outputs:
- output 1: bfloat16 [24576, 2048], P(('dp', 'sp')), parts along dimension 0
- output 2: bfloat16 [256, 1152, 2048], P(('dp', 'sp')), parts along dimension 0
There are 4 independent parts. A program takes and returns all parts, laid end to end along the dimension named above; an argument that names none is the same for every part.
All inputs are finite; a program needn't handle non-finite values.
Results may differ from a plain program's by a relative error of at most 0.00321.
Values are sent between devices in bfloat16 or wider.
A program may use at most 768 MiB of HBM per device.

v0:
```python
import math
import jax
import jax.numpy as jnp
from jax import lax
from jax.sharding import PartitionSpec as P

HEAD = 128
ROPE_BASE = 1000000.0


def rope(t, pos):
    half = t.shape[-1] // 2
    inv = ROPE_BASE ** (-jnp.arange(half, dtype=jnp.float32) * (2.0 / t.shape[-1]))
    ang = pos.astype(jnp.float32)[:, None] * inv[None, :]
    c = jnp.cos(ang)[:, None, :]
    s = jnp.sin(ang)[:, None, :]
    a = t[..., :half]
    b = t[..., half:]
    return jnp.concatenate([a * c - b * s, b * c + a * s], axis=-1)


def attend(q, kt, vt, qpos, last=None):
    sq_len, g, m, d = q.shape
    sk_len = kt.shape[1]
    lim = max(8, 2 ** int(math.log2(max(1, 2048 // (g * m)))))
    qb = math.gcd(sq_len, min(128, lim))
    nb = sq_len // qb
    scale = 1.0 / math.sqrt(d)
    qs = q.reshape(nb, qb, g, m, d).transpose(0, 2, 3, 1, 4)
    ps = qpos.reshape(nb, qb)
    kl = [sk_len] * nb
    if last is not None:
        gran = -(-sk_len // 8)
        kl = [min(sk_len, -(-(last(j * qb + qb - 1) + 1) // gran) * gran) for j in range(nb)]

    def run(qq, pp, n_k):
        kk = kt[:, :n_k]
        vv = vt[:, :n_k]
        kpos = jnp.arange(n_k)

        def block(a):
            qj, pj = a
            sc = jnp.einsum("gmqd,gkd->gmqk", qj, kk, preferred_element_type=jnp.float32) * scale
            keep = kpos[None, :] <= pj[:, None]
            sc = jnp.where(keep[None, None], sc, -jnp.inf)
            p = jax.nn.softmax(sc, axis=-1).astype(jnp.bfloat16)
            o = jnp.einsum("gmqk,gkd->gmqd", p, vv, preferred_element_type=jnp.float32)
            return o.astype(jnp.bfloat16)

        return lax.map(block, (qq, pp))

    outs = []
    j = 0
    while j < nb:
        e = j
        while e < nb and kl[e] == kl[j]:
            e += 1
        outs.append(run(qs[j:e], ps[j:e], kl[j]))
        j = e
    o = outs[0] if len(outs) == 1 else jnp.concatenate(outs, axis=0)
    return o.transpose(0, 3, 1, 2, 4).reshape(sq_len, g, m, d)


def route(idx, probs, cap):
    sd = idx.shape[0]
    ne = probs.shape[1]
    hot = idx[:, :, None] == jnp.arange(ne)[None, None, :]
    sel = jnp.sum(jnp.where(hot, probs[:, None, :], 0.0), axis=2)
    w = sel / jnp.sum(sel, axis=1, keepdims=True)
    gate = jnp.sum(jnp.where(hot, w[:, :, None], 0.0), axis=1)
    mine = jnp.any(hot, axis=1)
    tok = jnp.arange(sd)
    low = (tok[None, :] < tok[:, None]).astype(jnp.bfloat16)
    rank = jnp.dot(low, mine.astype(jnp.bfloat16), preferred_element_type=jnp.float32).astype(jnp.int32)
    pick = (rank.T[:, None, :] == jnp.arange(cap)[None, :, None]) & mine.T[:, None, :]
    ws = jnp.sum(jnp.where(pick, gate.T[:, None, :], 0.0), axis=2)
    return pick.astype(jnp.bfloat16), ws


def spread(h, pick, ws):
    hg = jnp.einsum("ect,th->ech", pick, h, preferred_element_type=jnp.bfloat16)
    return (ws[:, :, None] * hg.astype(jnp.float32)).astype(jnp.bfloat16)


def dispatch_rows(h, idx, probs, cap):
    pick, ws = route(idx, probs, cap)
    return spread(h, pick, ws)


def solution(mesh):
    n = mesh.shape["sp"]
    row = P(("dp", "sp"), None)
    full = P(None, None)

    def local(x, wq, wk, wv, wo, idx, probs):
        sd, hid = x.shape
        heads = wq.shape[1] // HEAD
        kvh = wk.shape[1] // HEAD
        m = heads // kvh
        ne = probs.shape[1]
        cap = 2 * sd * idx.shape[1] // ne
        me = lax.axis_index("sp")
        pos = me * sd + jnp.arange(sd)
        q = rope(jnp.dot(x, wq, preferred_element_type=jnp.float32).reshape(sd, heads, HEAD), pos)
        k = rope(jnp.dot(x, wk, preferred_element_type=jnp.float32).reshape(sd, kvh, HEAD), pos)
        q = q.astype(jnp.bfloat16).reshape(sd, heads * HEAD)
        k = k.astype(jnp.bfloat16).reshape(sd, kvh * HEAD)
        v = jnp.dot(x, wv, preferred_element_type=jnp.float32).astype(jnp.bfloat16)
        q = lax.all_to_all(q, "sp", 1, 0, tiled=True)
        k = lax.all_to_all(k, "sp", 1, 0, tiled=True)
        v = lax.all_to_all(v, "sp", 1, 0, tiled=True)
        s_len = n * sd
        g = kvh // n
        kt = k.reshape(s_len, g, HEAD).transpose(1, 0, 2)
        vt = v.reshape(s_len, g, HEAD).transpose(1, 0, 2)
        o = attend(q.reshape(s_len, g, m, HEAD), kt, vt, jnp.arange(s_len), lambda r: r)
        o = lax.all_to_all(o.reshape(s_len, g * m * HEAD), "sp", 0, 1, tiled=True)
        h = (x.astype(jnp.float32) + jnp.dot(o, wo, preferred_element_type=jnp.float32)).astype(jnp.bfloat16)
        send = dispatch_rows(h, idx, probs, cap)
        recv = lax.all_to_all(send, "sp", 0, 0, tiled=True)
        buf = recv.reshape(n, ne // n, cap, hid).transpose(1, 0, 2, 3).reshape(ne // n, n * cap, hid)
        return h, buf

    return jax.shard_map(local, mesh=mesh, in_specs=(row, full, full, full, full, row, row), out_specs=(row, P(("dp", "sp"), None, None)), check_vma=False)
```

profile of v0, /device:TPU:21, one launch (start us, length us, event | category | flops | bytes accessed | tf_op | source)
XLA Modules:
  0.0 789.3 jit_solution(8723925703313453776)
XLA Ops:
  0.6 7.3 fusion.127
  7.9 1.6 copy.121
  9.5 11.4 %all-to-all-start.2 = ((bf16[384,16,128]{2,0,1:T(8,128)(2,1)}), bf16[384,16,128]{2,0,1:T(8,128)(2,1)S(1)}, u32[]{:S(2)}, u32[]{:S(2)}) async-start(bf16[384,16,128]{2,0,1:T(8,128)(2,1)} %bitcast.248), calls=%async_computation.2 | async-start | bytes 3145728 | tf_op jit(solution)/shard_map/all_to_all | solution.py:111
  20.9 5.8 convolution_bitcast_fusion.1
  26.7 2.3 copy.110
  29.0 5.8 convolution_bitcast_fusion
  34.8 2.3 copy.111
  37.9 10.1 %fusion.137 = (f32[384,16,64]{2,1,0:T(8,128)S(1)}, f32[384,16,64]{2,1,0:T(8,128)}, f32[384,16,64]{2,1,0:T(8,128)}, f32[384,16,64]{2,1,0:T(8,128)}) fusion(f32[384,16,128]{2,1,0:T(8,128)} %bitcast.347, f32[384,16,128]{2,1,0:T(8,128)} %bitcast.346), kind=kLoop, calls=%fused_computation.189 | loop fusion | bytes 12582912 | tf_op jit(solution)/shard_map/slice | solution.py:17
  48.0 9.2 %subtract_convert_fusion = (bf16[384,16,64]{2,0,1:T(8,128)(2,1)S(1)}, bf16[384,16,64]{2,0,1:T(8,128)(2,1)S(1)}, bf16[384,16,64]{2,0,1:T(8,128)(2,1)}, bf16[384,16,64]{2,0,1:T(8,128)(2,1)}) fusion(f32[384,16,64]{2,1,0:T(8,128)} %get-tuple-element.633, f32[384,16,64]{2,1,0:T(8,128)S(1)} %get-tuple-element.632, f32[384,64]{1,0:T(8,128)S(1)} %get-tuple-element.655, ...), kind=kLoop, calls=%fused_computation.149 | loop fusion | flops 6291456 | bytes 9633792 | tf_op jit(solution)/shard_map/convert
  57.3 2.0 pad_maximum_fusion.1
  59.3 7.2 all-to-all-start.1
  66.5 3.9 pad_maximum_fusion
  70.4 34.4 %all-to-all-done.1 = bf16[384,16,128]{2,0,1:T(8,128)(2,1)S(1)} async-done(((bf16[384,16,128]{2,0,1:T(8,128)(2,1)}), bf16[384,16,128]{2,0,1:T(8,128)(2,1)S(1)}, u32[]{:S(2)}, u32[]{:S(2)}) %all-to-all-start.1) | async-done | bytes 1572896 | tf_op jit(solution)/shard_map/all_to_all | solution.py:110
  104.8 4.7 all-to-all-start
  121.6 25.7 %all-to-all-done = bf16[384,16,128]{2,0,1:T(8,128)(2,1)} async-done(((bf16[384,16,128]{2,0,1:T(8,128)(2,1)}), bf16[384,16,128]{2,0,1:T(8,128)(2,1)}, u32[]{:S(2)}, u32[]{:S(2)}) %all-to-all-start) | async-done | bytes 1572896 | tf_op jit(solution)/shard_map/all_to_all | solution.py:109
  147.3 2.6 fusion.139
  150.6 28.9 %while.94 = (s32[]{:T(128)}, bf16[6,1,1,128,128]{4,3,2,1,0:T(8,128)(2,1)}, s32[6,128]{1,0:T(8,128)}, bf16[6,1,1,128,128]{4,3,2,1,0:T(8,128)(2,1)}, bf16[1,5376,1...) while((s32[]{:T(128)}, bf16[6,1,1,128,128]{4,3,2,1,0:T(8,128)(2,1)}, ...), condition=%wide.region_27.28_spmd.clone, body=%wide.region_24.27_spmd.clone.sunk | while | flops 358530816 | bytes 16584829 | solution.py:50
  151.3 1.5 fusion.222
  156.1 1.5 fusion.222
  160.9 1.4 fusion.222
  163.7 1.3 fusion.224
  165.7 1.5 fusion.222
  168.5 1.3 fusion.224
  170.5 1.5 fusion.222
  173.3 1.3 fusion.224
  175.4 1.5 fusion.222
  178.2 1.3 fusion.224
  179.5 26.9 %while.95 = (s32[]{:T(128)}, bf16[6,1,1,128,128]{4,3,2,1,0:T(8,128)(2,1)S(1)}, s32[6,128]{1,0:T(8,128)}, bf16[6,1,1,128,128]{4,3,2,1,0:T(8,128)(2,1)}, bf16[1,61...) while((s32[]{:T(128)}, bf16[6,1,1,128,128]{4,3,2,1,0:T(8,128)(2,1)S(1)}, ...), condition=%wide.region_31.32_spmd.clone, body=%wide.region_28.31_spmd.clone.sunk | while | flops 409747200 | bytes 18944124 | solution.py:50
  180.3 1.5 fusion.227
  184.8 1.5 fusion.227
  189.3 1.5 fusion.227
  193.7 1.5 fusion.227
  198.2 1.5 fusion.227
  202.7 1.5 fusion.227
  206.5 24.2 %while.93 = (s32[]{:T(128)}, bf16[6,1,1,128,128]{4,3,2,1,0:T(8,128)(2,1)S(1)}, s32[6,128]{1,0:T(8,128)}, bf16[6,1,1,128,128]{4,3,2,1,0:T(8,128)(2,1)}, bf16[1,46...) while((s32[]{:T(128)}, bf16[6,1,1,128,128]{4,3,2,1,0:T(8,128)(2,1)S(1)}, ...), condition=%wide.region_23.24_spmd.clone, body=%wide.region_20.23_spmd.clone.sunk | while | flops 307314432 | bytes 14225533 | solution.py:50
  207.3 1.4 fusion.217
  211.3 1.4 fusion.217
  215.3 1.4 fusion.217
  219.3 1.4 fusion.217
  223.3 1.4 fusion.217
  227.4 1.4 fusion.217
  231.5 22.3 %while.92 = (s32[]{:T(128)}, bf16[6,1,1,128,128]{4,3,2,1,0:T(8,128)(2,1)}, s32[6,128]{1,0:T(8,128)}, bf16[6,1,1,128,128]{4,3,2,1,0:T(8,128)(2,1)}, bf16[1,3840,1...) while((s32[]{:T(128)}, bf16[6,1,1,128,128]{4,3,2,1,0:T(8,128)(2,1)}, ...), condition=%wide.region_19.20_spmd.clone, body=%wide.region_16.19_spmd.clone.sunk | while | flops 256098048 | bytes 11866237 | solution.py:50
  232.2 1.4 fusion.212
  235.9 1.4 fusion.212
  239.6 1.4 fusion.212
  243.3 1.4 fusion.212
  247.0 1.4 fusion.212
  250.7 1.4 fusion.212
  253.8 13.4 %while.91 = (s32[]{:T(128)}, bf16[6,1,1,128,128]{4,3,2,1,0:T(8,128)(2,1)S(1)}, s32[6,128]{1,0:T(8,128)S(1)}, bf16[6,1,1,128,128]{4,3,2,1,0:T(8,128)(2,1)}, bf16[...) while((s32[]{:T(128)}, ...), condition=%wide.region_15.16_spmd.clone, body=%wide.region_12.15_spmd.clone.sunk | while | flops 204881664 | bytes 9506941 | solution.py:50
  253.8 1.3 fusion.207
  256.0 1.3 fusion.207
  258.3 1.3 fusion.207
  260.5 1.3 fusion.207
  262.8 1.3 fusion.207
  267.3 12.3 %while.90 = (s32[]{:T(128)}, bf16[6,1,1,128,128]{4,3,2,1,0:T(8,128)(2,1)S(1)}, s32[6,128]{1,0:T(8,128)S(1)}, bf16[6,1,1,128,128]{4,3,2,1,0:T(8,128)(2,1)}, bf16[...) while((s32[]{:T(128)}, ...), condition=%wide.region_11.12_spmd.clone, body=%wide.region_8.11_spmd.clone.sunk | while | flops 153665280 | bytes 7147645 | solution.py:50
  279.6 10.7 %while.89 = (s32[]{:T(128)}, bf16[6,1,1,128,128]{4,3,2,1,0:T(8,128)(2,1)S(1)}, s32[6,128]{1,0:T(8,128)S(1)}, bf16[6,1,1,128,128]{4,3,2,1,0:T(8,128)(2,1)}, bf16[...) while((s32[]{:T(128)}, ...), condition=%wide.region_7.8_spmd.clone, body=%wide.region_4.7_spmd.clone.sunk | while | flops 102448896 | bytes 3215457 | solution.py:50
  290.5 9.9 %while.88 = (s32[]{:T(128)}, bf16[6,1,1,128,128]{4,3,2,1,0:T(8,128)(2,1)S(1)}, s32[6,128]{1,0:T(8,128)S(1)}, bf16[6,1,1,128,128]{4,3,2,1,0:T(8,128)(2,1)}, bf16[...) while((s32[]{:T(128)}, ...), condition=%wide.region_3.4_spmd.clone, body=%wide.region_0.3_spmd.clone.sunk | while | flops 51232512 | bytes 1642593 | solution.py:50
  305.9 5.0 all-to-all-start.3
  311.4 1.6 select_reduce_fusion
  313.1 35.8 %all-to-all-done.3 = bf16[16,384,128]{2,1,0:T(8,128)(2,1)S(1)} async-done(((bf16[16,384,128]{2,1,0:T(8,128)(2,1)}), bf16[16,384,128]{2,1,0:T(8,128)(2,1)S(1)}, u32[]{:S(2)}, u32[]{:S(2)}) %all-to-all-start.3) | async-done | bytes 1572896 | tf_op jit(solution)/shard_map/all_to_all | solution.py:117
  349.8 7.3 add_convert_fusion
  357.1 10.4 %multiply_convert_fusion = bf16[64,72,2048]{2,1,0:T(8,128)(2,1)S(1)} fusion(f32[64,72]{1,0:T(8,128)S(1)} %select_reduce_fusion, s32[64,384]{1,0:T(8,128)S(1)} %convolution_convert_fusion.6, pred[64,384]{1,0:T(8,128)(4,1)S(1)} %bitcast.361, bf16[384,2048]{1,0:T(8,128)(2,1)S(1)} %add_convert_fusion), kind=kOutput, calls=%fused_computation.141 | convolution fusion | flops 7279607808 | bytes 20588544 | tf_op jit(solution)/shard_map/ect,th->ech/dot_general | solution.py:81
  367.5 414.7 %all_to_all.66 = bf16[64,72,2048]{2,1,0:T(8,128)(2,1)S(1)} all-to-all(bf16[64,72,2048]{2,1,0:T(8,128)(2,1)S(1)} %multiply_convert_fusion), channel_id=1, replica_groups=mesh['dp'=4,'sp'=16] {'sp'}, dimensions={0} | all-to-all | bytes 37748736 | tf_op jit(solution)/shard_map/all_to_all | solution.py:120
  782.2 6.6 copy.104
  (305 shorter events, 122.1 us)
Async XLA Ops:
  9.5 11.4 %copy-start.20 = (bf16[384,2048]{1,0:T(8,128)(2,1)S(1)}, bf16[384,2048]{1,0:T(8,128)(2,1)}, u32[]{:S(2)}) copy-start(bf16[384,2048]{1,0:T(8,128)(2,1)} %param.23) | copy-start | bytes 4718596
  9.5 49.8 %all-to-all-start.2 = ((bf16[384,16,128]{2,0,1:T(8,128)(2,1)}), bf16[384,16,128]{2,0,1:T(8,128)(2,1)S(1)}, u32[]{:S(2)}, u32[]{:S(2)}) async-start(bf16[384,16,128]{2,0,1:T(8,128)(2,1)} %bitcast.248), calls=%async_computation.2 | async-start | bytes 3145728 | tf_op jit(solution)/shard_map/all_to_all | solution.py:111
  59.3 56.4 %copy-start.2 = (bf16[384,16,128]{2,0,1:T(8,128)(2,1)}, bf16[384,16,128]{2,0,1:T(8,128)(2,1)S(1)}, u32[]{:S(2)}) copy-start(bf16[384,16,128]{2,0,1:T(8,128)(2,1)S(1)} %all-to-all-done.2) | copy-start | bytes 4718596
  59.3 45.5 %all-to-all-start.1 = ((bf16[384,16,128]{2,0,1:T(8,128)(2,1)}), bf16[384,16,128]{2,0,1:T(8,128)(2,1)S(1)}, u32[]{:S(2)}, u32[]{:S(2)}) async-start(bf16[384,16,128]{2,0,1:T(8,128)(2,1)} %pad_maximum_fusion.1), calls=%async_computation.1 | async-start | bytes 3145728 | tf_op jit(solution)/shard_map/all_to_all | solution.py:110
  104.8 42.4 %all-to-all-start = ((bf16[384,16,128]{2,0,1:T(8,128)(2,1)}), bf16[384,16,128]{2,0,1:T(8,128)(2,1)}, u32[]{:S(2)}, u32[]{:S(2)}) async-start(bf16[384,16,128]{2,0,1:T(8,128)(2,1)} %pad_maximum_fusion), calls=%async_computation | async-start | bytes 3145728 | tf_op jit(solution)/shard_map/all_to_all | solution.py:109
  152.8 1.3 copy-start.7
  157.6 1.3 copy-start.7
  162.4 1.3 copy-start.7
  167.2 1.3 copy-start.7
  172.0 1.3 copy-start.7
  176.8 1.3 copy-start.7
  179.5 27.0 %copy-start = (bf16[1,4608,128]{2,1,0:T(8,128)(2,1)S(1)}, bf16[1,4608,128]{2,1,0:T(8,128)(2,1)}, u32[]{:S(2)}) copy-start(bf16[1,4608,128]{2,1,0:T(8,128)(2,1)} %slice.194) | copy-start | bytes 3538948
  181.8 1.4 copy-start.3
  186.3 1.4 copy-start.3
  190.8 1.4 copy-start.3
  195.3 1.4 copy-start.3
  199.7 1.4 copy-start.3
  204.2 1.4 copy-start.3
  206.5 25.0 %copy-start.1 = (bf16[1,3840,128]{2,1,0:T(8,128)(2,1)S(1)}, bf16[1,3840,128]{2,1,0:T(8,128)(2,1)}, u32[]{:S(2)}) copy-start(bf16[1,3840,128]{2,1,0:T(8,128)(2,1)} %slice.190) | copy-start | bytes 2949124
  208.7 1.3 copy-start.8
  212.7 1.3 copy-start.8
  216.7 1.3 copy-start.8
  220.7 1.3 copy-start.8
  224.7 1.3 copy-start.8
  228.8 1.3 copy-start.8
  230.7 0.7 copy-start.12
  231.5 22.3 %copy-start.4 = (bf16[1,3072,128]{2,1,0:T(8,128)(2,1)S(1)}, bf16[1,3072,128]{2,1,0:T(8,128)(2,1)}, u32[]{:S(2)}) copy-start(bf16[1,3072,128]{2,1,0:T(8,128)(2,1)} %slice.186) | copy-start | bytes 2359300
  232.2 1.8 copy-start.9
  235.9 1.8 copy-start.9
  239.6 1.8 copy-start.9
  243.3 1.8 copy-start.9
  247.0 1.8 copy-start.9
  250.7 1.8 copy-start.9
  253.8 1.7 copy-start.10
  256.0 1.7 copy-start.10
  258.3 1.7 copy-start.10
  260.5 1.7 copy-start.10
  262.8 1.7 copy-start.10
  265.0 1.7 copy-start.10
  267.2 12.4 %copy-start.5 = (bf16[1,1536,128]{2,1,0:T(8,128)(2,1)S(1)}, bf16[1,1536,128]{2,1,0:T(8,128)(2,1)}, u32[]{:S(2)}) copy-start(bf16[1,1536,128]{2,1,0:T(8,128)(2,1)} %slice.178) | copy-start | bytes 1179652
  267.3 12.4 %copy-start.16 = (bf16[1,1536,128]{2,1,0:T(8,128)(2,1)S(1)}, bf16[1,1536,128]{2,1,0:T(8,128)(2,1)}, u32[]{:S(2)}) copy-start(bf16[1,1536,128]{2,1,0:T(8,128)(2,1)} %slice.179) | copy-start | bytes 1179652
  267.3 1.6 copy-start.15
  269.4 1.6 copy-start.15
  271.4 1.6 copy-start.15
  273.4 1.6 copy-start.15
  275.5 1.6 copy-start.15
  277.5 1.6 copy-start.15
  279.6 10.8 %copy-start.6 = (bf16[1,768,128]{2,1,0:T(8,128)(2,1)S(1)}, bf16[1,768,128]{2,1,0:T(8,128)(2,1)}, u32[]{:S(2)}) copy-start(bf16[1,768,128]{2,1,0:T(8,128)(2,1)} %slice.174) | copy-start | bytes 589828
  279.6 10.8 %copy-start.17 = (bf16[1,768,128]{2,1,0:T(8,128)(2,1)S(1)}, bf16[1,768,128]{2,1,0:T(8,128)(2,1)}, u32[]{:S(2)}) copy-start(bf16[1,768,128]{2,1,0:T(8,128)(2,1)} %slice.175) | copy-start | bytes 589828
  290.4 12.7 %copy-start.14 = (bf16[6,1,1,128,128]{4,3,2,1,0:T(8,128)(2,1)S(1)}, bf16[6,1,1,128,128]{4,3,2,1,0:T(8,128)(2,1)}, u32[]{:S(2)}) copy-start(bf16[6,1,1,128,128]{4,3,2,1,0:T(8,128)(2,1)} %get-tuple-element.302) | copy-start | bytes 589828
  300.4 3.5 copy-start.13
  300.4 4.2 copy-start.11
  304.5 6.4 copy-start.18
  304.5 6.5 copy-start.19
  305.9 43.0 %all-to-all-start.3 = ((bf16[16,384,128]{2,1,0:T(8,128)(2,1)}), bf16[16,384,128]{2,1,0:T(8,128)(2,1)S(1)}, u32[]{:S(2)}, u32[]{:S(2)}) async-start(bf16[16,384,128]{2,1,0:T(8,128)(2,1)} %bitcast.31), calls=%async_computation.3 | async-start | bytes 3145728 | tf_op jit(solution)/shard_map/all_to_all | solution.py:117
  357.1 10.4 %copy-start.21 = (bf16[384,2048]{1,0:T(8,128)(2,1)}, bf16[384,2048]{1,0:T(8,128)(2,1)S(1)}, u32[]{:S(2)}) copy-start(bf16[384,2048]{1,0:T(8,128)(2,1)S(1)} %add_convert_fusion) | copy-start | bytes 4718596
where the time goes:
time: 796 us; the launch traced here: 789 us
  blocking collectives  415 us (52%)
  matrix products  133 us (17%)
  waiting for transfers between devices  95.9 us (12%)
  local copies, waits for them, and re-layouts  77.1 us (10%)
  other arithmetic  37.1 us (5%)
  starting transfers between devices  28.3 us (4%)
    all_to_all x1, blocking collectives, local(): recv = lax.all_to_all(send, 'sp', 0, 0, tiled=True)  415 us
    dot_general x48, matrix products, block(): jnp.einsum('gmqd,gkd->gmqk', qj, kk, preferred_element_type=jnp.float32)  63.3 us
    all_to_all x1, waiting for transfers between devices, local(): o = lax.all_to_all(o.reshape(s_len, g * m * HEAD), 'sp', 0, 1, tiled=True)  35.8 us
    all_to_all x1, waiting for transfers between devices, local(): k = lax.all_to_all(k, 'sp', 1, 0, tiled=True)  34.4 us
    dot_general x48, matrix products, block(): o = jnp.einsum('gmqk,gkd->gmqd', p, vv, preferred_element_type=jnp.float32)  33.2 us
    all_to_all x1, waiting for transfers between devices, local(): q = lax.all_to_all(q, 'sp', 1, 0, tiled=True)  25.7 us
    reduce_sum x48, other arithmetic, block(): p = jax.nn.softmax(sc, axis=-1).astype(jnp.bfloat16)  19.2 us
    le x48, local copies, waits for them, and re-layouts, block(): keep = kpos[None, :] <= pj[:, None]  16.9 us
  transfers between devices with their start and end apart: 4, of which 3 were waited for; matrix products, arithmetic and copies ran while one was open for 7% of the time, Pallas kernels for 0%

commit v1 on v0

v1 whole, which is shorter than its diff:
```python
import functools
import math
import jax
import jax.numpy as jnp
from jax import lax
from jax.experimental import pallas as pl
from jax.experimental.pallas import tpu as pltpu
from jax.sharding import PartitionSpec as P

HEAD = 128
ROPE_BASE = 1000000.0
MESH = pl.DeviceIdType.MESH
ANY = pl.BlockSpec(memory_space=pl.ANY)
VM = pl.BlockSpec(memory_space=pltpu.VMEM)
DMA = pltpu.SemaphoreType.DMA
VMEM_BYTES = 64 * 1024 * 1024 - 64 * 1024


class Ring:
    def __init__(self, n):
        self.chips = n // 2
        self.half = self.chips // 2
        self.me = lax.axis_index("sp")
        self.z = self.me // 2
        self.c = self.me % 2
        self.right = self.at(1)
        self.left = self.at(-1)
        self.part = self.z * 2 + 1 - self.c

    def at(self, d, other=False):
        c = 1 - self.c if other else self.c
        return lax.rem(self.z + self.chips + d, self.chips) * 2 + c

    def barrier(self):
        bar = pltpu.get_barrier_semaphore()
        for dev in (self.right, self.left, self.part):
            pl.semaphore_signal(bar, inc=1, device_id={"sp": dev}, device_id_type=MESH)
        pl.semaphore_wait(bar, 3)


def remote(src, dst, ss, rs, dev):
    return pltpu.make_async_remote_copy(src_ref=src, dst_ref=dst, send_sem=ss, recv_sem=rs, device_id={"sp": dev}, device_id_type=MESH)


def gather_project(n, pieces, x, wq, wk, wv, inv, meta, xf, qo, ko, vo, mo, xs, wb, qs, ks, vs, ms, cws, cwr, ccs, ccr, pts, ptr, wsem, osem):
    r = Ring(n)
    me, half = r.me, r.half
    sd, hid = x.shape
    rows = sd // pieces
    cols = pl.ds(pl.multiple_of(me * HEAD, HEAD), HEAD)
    own = [pltpu.make_async_copy(w.at[:, cols], wb.at[:, pl.ds(i * HEAD, HEAD)], wsem.at[i]) for i, w in enumerate((wq, wk, wv))]
    own.append(pltpu.make_async_copy(x, xs.at[me], wsem.at[3]))
    own.append(pltpu.make_async_copy(meta, ms.at[me], wsem.at[4]))
    for cp in own:
        cp.start()
    r.barrier()

    def blk(chunk, p):
        return ms.at[chunk] if p == pieces else xs.at[chunk, pl.ds(p * rows, rows)]

    def src(p):
        return meta if p == pieces else x.at[pl.ds(p * rows, rows)]

    sent = []

    def go(cp):
        cp.start()
        sent.append(cp)

    order = [pieces] + list(range(pieces))

    def takes(d, p, cw):
        if d < half:
            return True
        return d == half and (cw if p == pieces else (p < pieces // 2) == cw)

    for p in order:
        go(remote(src(p), blk(me, p), cws.at[0, p], cwr.at[0, p], r.right))
        go(remote(src(p), blk(me, p), ccs.at[0, p], ccr.at[0, p], r.left))
        go(remote(src(p), blk(me, p), pts.at[0, p], ptr.at[0, p], r.part))

    outs = []

    def out(src_, dst, i, slot):
        cp = pltpu.make_async_copy(src_, dst, osem.at[i, slot])
        cp.start()
        outs.append(cp)

    def project(chunk, slot):
        out(xs.at[chunk], xf.at[chunk], 0, slot)
        acc = jnp.dot(xs[chunk], wb[...], preferred_element_type=jnp.float32)
        pos = (chunk * sd + lax.broadcasted_iota(jnp.int32, (sd, HEAD), 0)).astype(jnp.float32)
        ang = pos * inv[...]
        co = jnp.cos(ang)
        si = jnp.sin(ang)
        si = jnp.where(lax.broadcasted_iota(jnp.int32, (sd, HEAD), 1) < HEAD // 2, -si, si)
        q = acc[:, :HEAD]
        k = acc[:, HEAD : 2 * HEAD]
        qs[chunk] = (q * co + pltpu.roll(q, HEAD // 2, 1) * si).astype(jnp.bfloat16)
        ks[chunk] = (k * co + pltpu.roll(k, HEAD // 2, 1) * si).astype(jnp.bfloat16)
        vs[chunk] = acc[:, 2 * HEAD :].astype(jnp.bfloat16)
        out(qs.at[chunk], qo.at[chunk], 1, slot)
        out(ks.at[chunk], ko.at[chunk], 2, slot)
        out(vs.at[chunk], vo.at[chunk], 3, slot)

    for cp in own:
        cp.wait()
    project(me, 0)
    slot = 1
    waiting = [(r.part, 0, order)]
    for d in range(1, half + 1):
        a, b = r.at(-d), r.at(d)
        s1 = 2 * d - 1
        s2 = 2 * d if d < half else s1
        for p in order:
            if takes(d, p, True):
                remote(blk(a, p), blk(a, p), cws.at[d - 1, p], cwr.at[d - 1, p], r.right).wait_recv()
                if takes(d + 1, p, True):
                    go(remote(blk(a, p), blk(a, p), cws.at[d, p], cwr.at[d, p], r.right))
                go(remote(blk(a, p), blk(a, p), pts.at[s1, p], ptr.at[s1, p], r.part))
            if takes(d, p, False):
                remote(blk(b, p), blk(b, p), ccs.at[d - 1, p], ccr.at[d - 1, p], r.left).wait_recv()
                if takes(d + 1, p, False):
                    go(remote(blk(b, p), blk(b, p), ccs.at[d, p], ccr.at[d, p], r.left))
                go(remote(blk(b, p), blk(b, p), pts.at[s2, p], ptr.at[s2, p], r.part))
        for chunk in (a, b) if d < half else (a,):
            project(chunk, slot)
            slot += 1
        for chunk, s, ps in waiting:
            for p in ps:
                remote(blk(chunk, p), blk(chunk, p), pts.at[s, p], ptr.at[s, p], r.part).wait_recv()
            project(chunk, slot)
            slot += 1
        ao, bo = r.at(-d, True), r.at(d, True)
        waiting = [(ao, s1, order), (bo, s2, order)] if d < half else [(ao, s1, order)]
    for chunk, s, ps in waiting:
        for p in ps:
            remote(blk(chunk, p), blk(chunk, p), pts.at[s, p], ptr.at[s, p], r.part).wait_recv()
        project(chunk, slot)
        slot += 1
    last = pltpu.make_async_copy(ms, mo, wsem.at[5])
    last.start()
    for cp in sent:
        cp.wait_send()
    for cp in outs:
        cp.wait()
    last.wait()


def call_gather_project(x, wq, wk, wv, inv, meta, n, pieces=4):
    sd, hid = x.shape
    half = n // 4
    bf = jnp.bfloat16
    head = jax.ShapeDtypeStruct((n, sd, HEAD), bf)
    return pl.pallas_call(
        functools.partial(gather_project, n, pieces),
        out_shape=(jax.ShapeDtypeStruct((n, sd, hid), bf), head, head, head, jax.ShapeDtypeStruct((n,) + meta.shape, meta.dtype)),
        in_specs=[ANY, ANY, ANY, ANY, VM, ANY],
        out_specs=(ANY,) * 5,
        scratch_shapes=[
            pltpu.VMEM((n, sd, hid), bf),
            pltpu.VMEM((hid, 3 * HEAD), bf),
            pltpu.VMEM((n, sd, HEAD), bf),
            pltpu.VMEM((n, sd, HEAD), bf),
            pltpu.VMEM((n, sd, HEAD), bf),
            pltpu.VMEM((n,) + meta.shape, meta.dtype),
        ]
        + [DMA((half, pieces + 1))] * 4
        + [DMA((2 * half, pieces + 1))] * 2
        + [DMA((6,)), DMA((4, n))],
        compiler_params=pltpu.CompilerParams(collective_id=1, has_side_effects=True, vmem_limit_bytes=VMEM_BYTES),
        name="gather_project",
    )(x, wq, wk, wv, inv, meta)


def attend_block(i, q, kb, vb, m, l, acc, scale):
    bq = q.shape[0]
    bk = 2 * bq
    sub = 128
    c = scale * math.log2(math.e)
    m[...] = jnp.full(m.shape, -jnp.inf, jnp.float32)
    l[...] = jnp.zeros(l.shape, jnp.float32)
    acc[...] = jnp.zeros(acc.shape, jnp.float32)

    def step(j, masked):
        ks = kb[pl.ds(pl.multiple_of(j * bk, bk), bk), :]
        vs = vb[pl.ds(pl.multiple_of(j * bk, bk), bk), :]
        for t in range(bq // sub):
            rows = pl.ds(t * sub, sub)
            s = lax.dot_general(q[rows, :], ks, (((1,), (1,)), ((), ())), preferred_element_type=jnp.float32)
            if masked:
                qp = i * bq + t * sub + lax.broadcasted_iota(jnp.int32, (sub, bk), 0)
                kp = j * bk + lax.broadcasted_iota(jnp.int32, (sub, bk), 1)
                s = jnp.where(kp <= qp, s, -jnp.inf)
            top = jnp.max(s, axis=1, keepdims=True)
            old = m[rows, :]
            new = jnp.maximum(old, top)
            p = jnp.exp2(s * c - new[:, :1] * c)
            alpha = jnp.exp2((old - new) * c)
            part = p[:, :HEAD]
            for g in range(1, bk // HEAD):
                part = part + p[:, g * HEAD : (g + 1) * HEAD]
            l[rows, :] = l[rows, :] * alpha + part
            acc[rows, :] = acc[rows, :] * alpha + jnp.dot(p.astype(jnp.bfloat16), vs, preferred_element_type=jnp.float32)
            m[rows, :] = new

    def body(j, carry):
        step(j, False)
        return carry

    lax.fori_loop(0, i // 2, body, 0)
    step(i // 2, True)
    return (acc[...] / jnp.sum(l[...], axis=1, keepdims=True)).astype(jnp.bfloat16)


def attend_gather(n, q, k, v, xf, wo, hf, o, wb, qb, kb, vb, xb, hb, m, l, acc, cws, cwr, ccs, ccr, pts, ptr, lsem, xsem, hsem):
    r = Ring(n)
    me, half = r.me, r.half
    nb, _, bq, _ = o.shape
    hid = wo.shape[1]
    cut = bq // 2
    tile = 512
    scale = 1.0 / math.sqrt(HEAD)
    load = [pltpu.make_async_copy(a, b, lsem.at[i]) for i, (a, b) in enumerate(((q, qb), (k, kb), (v, vb), (wo, wb)))]
    for cp in load:
        cp.start()
    pltpu.make_async_copy(xf.at[0], xb.at[0], xsem.at[0]).start()
    r.barrier()
    for cp in load[:3]:
        cp.wait()

    lo, hi, whole = pl.ds(0, cut), pl.ds(cut, cut), pl.ds(0, bq)

    def cw(b, d):
        chunk = r.at(-d)
        ref = o.at[b, chunk, lo if d + 1 == half else whole]
        return remote(ref, ref, cws.at[d, b], cwr.at[d, b], r.right)

    def ccw(b, d):
        chunk = r.at(d)
        ref = o.at[b, chunk, hi if d + 1 == half else whole]
        return remote(ref, ref, ccs.at[d, b], ccr.at[d, b], r.left)

    def cw_in(b, d):
        ref = o.at[b, r.at(-d), lo if d == half else whole]
        return remote(ref, ref, cws.at[d - 1, b], cwr.at[d - 1, b], r.right)

    def ccw_in(b, d):
        ref = o.at[b, r.at(d), hi if d == half else whole]
        return remote(ref, ref, ccs.at[d - 1, b], ccr.at[d - 1, b], r.left)

    def cross(b, s, other):
        d = (s + 1) // 2
        sign = -1 if s % 2 == 1 else 1
        rows = whole if d < half else (lo if sign < 0 else hi)
        ref = o.at[b, r.at(sign * d, other), rows]
        return remote(ref, ref, pts.at[s, b], ptr.at[s, b], r.part)

    def attend(i):
        o[i, me] = attend_block(i, qb.at[pl.ds(pl.multiple_of(i * bq, bq), bq)], kb, vb, m, l, acc, scale)

    def project(b):
        @pl.when(b + 1 < nb)
        def _():
            pltpu.make_async_copy(xf.at[b + 1], xb.at[(b + 1) % 2], xsem.at[(b + 1) % 2]).start()

        pltpu.make_async_copy(xf.at[b], xb.at[b % 2], xsem.at[b % 2]).wait()

        @pl.when(b >= 2)
        def _():
            pltpu.make_async_copy(hb.at[b % 2], hf.at[b - 2], hsem.at[b % 2]).wait()

        def cols(t, carry):
            at = pl.ds(pl.multiple_of(t * tile, tile), tile)
            lhs = jnp.concatenate([o[b, j] for j in range(n)], axis=1)
            y = jnp.dot(lhs, wb[:, at], preferred_element_type=jnp.float32)
            hb[b % 2, :, at] = (xb[b % 2, :, at].astype(jnp.float32) + y).astype(jnp.bfloat16)
            return carry

        lax.fori_loop(0, hid // tile, cols, 0)
        pltpu.make_async_copy(hb.at[b % 2], hf.at[b], hsem.at[b % 2]).start()

    attend(0)
    load[3].wait()

    def step(i, carry):
        @pl.when(i < nb)
        def _():
            cw(i, 0).start()
            ccw(i, 0).start()
            cross(i, 0, False).start()

        for d in range(half, 0, -1):
            b = i - d

            @pl.when(jnp.logical_and(b >= 0, b < nb))
            def _(d=d, b=b):
                cw_in(b, d).wait_recv()
                if d < half:
                    cw(b, d).start()
                cross(b, 2 * d - 1, False).start()
                ccw_in(b, d).wait_recv()
                if d < half:
                    ccw(b, d).start()
                cross(b, 2 * d, False).start()

        @pl.when(i + 1 < nb)
        def _():
            attend(i + 1)

        b = i - half - 1

        @pl.when(b >= 0)
        def _():
            for s in range(2 * half + 1):
                cross(b, s, True).wait_recv()
            project(b)

        return carry

    lax.fori_loop(0, nb + half + 1, step, 0)

    def drain(b, carry):
        for d in range(half):
            cw(b, d).wait_send()
            ccw(b, d).wait_send()
        for s in range(2 * half + 1):
            cross(b, s, False).wait_send()
        return carry

    lax.fori_loop(0, nb, drain, 0)
    for b in (nb - 2, nb - 1):
        pltpu.make_async_copy(hb.at[b % 2], hf.at[b], hsem.at[b % 2]).wait()


def call_attend_gather(q, k, v, xf, wo, n):
    nb, sd, hid = xf.shape
    half = n // 4
    s = nb * sd
    bf, f32 = jnp.bfloat16, jnp.float32
    return pl.pallas_call(
        functools.partial(attend_gather, n),
        out_shape=jax.ShapeDtypeStruct((nb, sd, hid), bf),
        in_specs=[ANY] * 5,
        out_specs=ANY,
        scratch_shapes=[
            pltpu.VMEM((nb, n, sd, HEAD), bf),
            pltpu.VMEM(wo.shape, bf),
            pltpu.VMEM((s, HEAD), bf),
            pltpu.VMEM((s, HEAD), bf),
            pltpu.VMEM((s, HEAD), bf),
            pltpu.VMEM((2, sd, hid), bf),
            pltpu.VMEM((2, sd, hid), bf),
            pltpu.VMEM((sd, HEAD), f32),
            pltpu.VMEM((sd, HEAD), f32),
            pltpu.VMEM((sd, HEAD), f32),
        ]
        + [DMA((half, nb))] * 4
        + [DMA((2 * half + 1, nb))] * 2
        + [DMA((4,)), DMA((2,)), DMA((2,))],
        compiler_params=pltpu.CompilerParams(collective_id=2, has_side_effects=True, vmem_limit_bytes=VMEM_BYTES),
        name="attend_gather",
    )(q, k, v, xf, wo)


def dispatch(cap, per, meta, hf, h_own, buf):
    s = pl.program_id(0)
    me = lax.axis_index("sp")
    sd = hf.shape[1]
    kp = meta.shape[1] // 2
    chosen, gates = meta[0, :kp, :], meta[0, kp:, :]
    mine, gate = [], []
    for j in range(per):
        hit = chosen == (me * per + j).astype(jnp.float32)
        mine.append(jnp.max(jnp.where(hit, 1.0, 0.0), axis=0, keepdims=True))
        gate.append(jnp.sum(jnp.where(hit, gates, 0.0), axis=0, keepdims=True))
    low = lax.broadcasted_iota(jnp.int32, (sd, sd), 0) < lax.broadcasted_iota(jnp.int32, (sd, sd), 1)
    every = jnp.concatenate(mine + [jnp.zeros((8 - per, sd), jnp.float32)], axis=0).astype(jnp.bfloat16)
    rank = jnp.dot(every, jnp.where(low, 1.0, 0.0).astype(jnp.bfloat16), preferred_element_type=jnp.float32)
    place = lax.broadcasted_iota(jnp.int32, (cap, sd), 0).astype(jnp.float32)
    picks, ws = [], []
    for j in range(per):
        at = jnp.where(mine[j] > 0.5, rank[j : j + 1, :], -1.0) == place
        picks.append(jnp.where(at, 1.0, 0.0))
        ws.append(jnp.sum(jnp.where(at, gate[j], 0.0), axis=1, keepdims=True))
    pick = jnp.concatenate(picks, axis=0).astype(jnp.bfloat16)
    w = jnp.concatenate(ws, axis=0)
    hid = hf.shape[2]
    tile = 512
    for t in range(hid // tile):
        cols = pl.ds(t * tile, tile)
        rows = w * jnp.dot(pick, hf[0, :, cols], preferred_element_type=jnp.float32)
        for j in range(per):
            buf[j, :, cols] = rows[j * cap : (j + 1) * cap, :].astype(jnp.bfloat16)

    @pl.when(s == me)
    def _():
        h_own[...] = hf[0]


def call_dispatch(meta, hf, cap, per):
    n, sd, hid = hf.shape
    return pl.pallas_call(
        functools.partial(dispatch, cap, per),
        grid=(n,),
        out_shape=(jax.ShapeDtypeStruct((sd, hid), jnp.bfloat16), jax.ShapeDtypeStruct((per, n * cap, hid), jnp.bfloat16)),
        in_specs=[pl.BlockSpec((1,) + meta.shape[1:], lambda s: (s, 0, 0)), pl.BlockSpec((1, sd, hid), lambda s: (s, 0, 0))],
        out_specs=(pl.BlockSpec((sd, hid), lambda s: (0, 0)), pl.BlockSpec((per, cap, hid), lambda s: (0, s, 0))),
        compiler_params=pltpu.CompilerParams(dimension_semantics=("arbitrary",), vmem_limit_bytes=48 * 1024 * 1024),
        name="dispatch",
    )(meta, hf)


def routing(idx, probs):
    top = idx.shape[1]
    pad = -top % 8
    hot = idx[:, :, None] == jnp.arange(probs.shape[1])[None, None, :]
    sel = jnp.sum(jnp.where(hot, probs[:, None, :], 0.0), axis=2)
    w = sel / jnp.sum(sel, axis=1, keepdims=True)
    e = jnp.pad(idx.astype(jnp.float32), ((0, 0), (0, pad)), constant_values=-1.0)
    return jnp.concatenate([e, jnp.pad(w, ((0, 0), (0, pad)))], axis=1).T


def solution(mesh):
    n = mesh.shape["sp"]
    row = P(("dp", "sp"), None)
    full = P(None, None)

    def local(x, wq, wk, wv, wo, idx, probs):
        sd, hid = x.shape
        ne = probs.shape[1]
        cap = 2 * sd * idx.shape[1] // ne
        inv = ROPE_BASE ** (-jnp.arange(HEAD // 2, dtype=jnp.float32) * (2.0 / HEAD))
        inv = jnp.concatenate([inv, inv])[None, :]
        meta = routing(idx, probs)
        xf, q, k, v, metas = call_gather_project(x, wq, wk, wv, inv, meta, n)
        q, k, v = (a.reshape(n * sd, HEAD) for a in (q, k, v))
        hf = call_attend_gather(q, k, v, xf, wo, n)
        h, buf = call_dispatch(metas, hf, cap, ne // n)
        return h, buf

    return jax.shard_map(local, mesh=mesh, in_specs=(row, full, full, full, full, row, row), out_specs=(row, P(("dp", "sp"), None, None)), check_vma=False)
```

time: 796 us -> 368 us (0.46)
  blocking collectives: 415 us -> 0 us
  Pallas kernels: 0 us -> 361 us
  matrix products: 133 us -> 0 us
  waiting for transfers between devices: 95.9 us -> 0 us
  local copies, waits for them, and re-layouts: 77.1 us -> 0.99 us
  other arithmetic: 37.1 us -> 2.94 us
  starting transfers between devices: 28.3 us -> 0 us
    all_to_all x1 -> x0, blocking collectives: 415 us -> none  [local(): recv = lax.all_to_all(send, 'sp', 0, 0, tiled=True)]
    pallas_call x0 -> x3, Pallas kernels: none -> 361 us  [the longest x1 196 us: call_attend_gather(): pl.pallas_call(functools.partial(attend_gather, n), out_shape=jax.ShapeDt...]
    dot_general x102 -> x0, matrix products: 133 us -> none  [the longest x48 63.3 us: block(): jnp.einsum('gmqd,gkd->gmqk', qj, kk, preferred_element_type=jnp.float32)]
    all_to_all x4 -> x0, waiting for transfers between devices: 95.9 us -> none  [the longest x1 35.8 us: local(): o = lax.all_to_all(o.reshape(s_len, g * m * HEAD), 'sp', 0, 1, tiled=True)]
    all_to_all x4 -> x0, starting transfers between devices: 28.3 us -> none  [the longest x1 11.4 us: local(): v = lax.all_to_all(v, 'sp', 1, 0, tiled=True)]
    slice x17 -> x0, local copies, waits for them, and re-layouts: 24.7 us -> none  [the longest x1 10.1 us: rope(): a = t[..., :half]]
    reduce_sum x51 -> x1, other arithmetic: 21 us -> 1.01 us  [routing(): w = sel / jnp.sum(sel, axis=1, keepdims=True)]
    le x48 -> x0, local copies, waits for them, and re-layouts: 16.9 us -> none  [block(): keep = kpos[None, :] <= pj[:, None]]
  transfers between devices with their start and end apart: 4 -> 0, of which waited for: 3 -> 0; matrix products, arithmetic and copies ran while one was open for 7% -> 0% of each run, Pallas kernels for 0% -> 0%
where the time goes in v1:
time: 368 us; the launch traced here: 365 us
  Pallas kernels  361 us (98%)
    pallas_call x1, Pallas kernels, call_attend_gather(): pl.pallas_call(functools.partial(attend_gather, n), out_shape=jax.ShapeDt...  196 us
    pallas_call x1, Pallas kernels, call_gather_project(): pl.pallas_call(functools.partial(gather_project, n, pieces), out_shape=(j...  139 us
    pallas_call x1, Pallas kernels, call_dispatch(): pl.pallas_call(functools.partial(dispatch, cap, per), grid=(n,), out_shap...  25.4 us

profile of v1, /device:TPU:21, one launch (start us, length us, event | category | flops | bytes accessed | tf_op | source)
XLA Modules:
  0.0 365.2 jit_solution(18130123862171156586)
XLA Ops:
  0.6 0.6 maximum_bitcast_fusion.inv
  1.2 0.7 convert_element_type.5
  1.9 1.0 select_reduce_fusion
  3.0 0.6 fusion.meta
  3.6 139.1 %gather_project.1 = (bf16[16,384,2048]{2,1,0:T(8,128)(2,1)}, bf16[16,384,128]{2,1,0:T(8,128)(2,1)}, bf16[16,384,128]{2,1,0:T(8,128)(2,1)}, bf16[16,384,128]{2,1,0:T(8,128)(2,1)}, f32[16,16,384]{2,1,0:T(8,128)}) custom-call(bf16[384,2048]{1,0:T(8,128)(2,1)} %x.5, bf16[2048,2048]{1,0:T(8,128)(2,1)} %wq.1, bf16[2048,2048]{1,0:T(8,128)(2,1)} %wk.1, ...), custom_call_target="tpu_custom_call" | custom-call | tf_op jit(solution)/shard_map/gather_project/pallas_call | solution.py:155
  142.7 196.2 %attend_gather.1.hf = bf16[16,384,2048]{2,1,0:T(8,128)(2,1)} custom-call(bf16[6144,128]{1,0:T(8,128)(2,1)} %bitcast.7, bf16[6144,128]{1,0:T(8,128)(2,1)} %bitcast.8, bf16[6144,128]{1,0:T(8,128)(2,1)} %bitcast.9, bf16[16,384,2048]{2,1,0:T(8,128)(2,1)} %get-tuple-element.11.xf, bf16[2048,2048]{1,0:T(8,128)(2,1)} %wo.1), custom_call_target="tpu_custom_call" | custom-call | tf_op jit(solution)/shard_map/attend_gather/pallas_call | solution.py:341
  338.9 0.0 copy-start
  338.9 1.0 copy-done
  339.9 25.4 %dispatch.1 = (bf16[384,2048]{1,0:T(8,128)(2,1)}, bf16[4,1152,2048]{2,1,0:T(8,128)(2,1)}) custom-call(f32[16,16,384]{2,1,0:T(8,128)S(1)} %copy-done, bf16[16,384,2048]{2,1,0:T(8,128)(2,1)} %attend_gather.1.hf), custom_call_target="tpu_custom_call" | custom-call | tf_op jit(solution)/shard_map/dispatch/pallas_call | solution.py:403
  (2 shorter events, 0.0 us)
Async XLA Ops:
  338.9 1.0 copy-start

commit v2 on v1

v2 whole, which is shorter than its diff:
```python
import functools
import math
import jax
import jax.numpy as jnp
from jax import lax
from jax.experimental import pallas as pl
from jax.experimental.pallas import tpu as pltpu
from jax.sharding import PartitionSpec as P

HEAD = 128
ROPE_BASE = 1000000.0
MESH = pl.DeviceIdType.MESH
ANY = pl.BlockSpec(memory_space=pl.ANY)
VM = pl.BlockSpec(memory_space=pltpu.VMEM)
DMA = pltpu.SemaphoreType.DMA
VMEM_BYTES = 64 * 1024 * 1024 - 64 * 1024


class Ring:
    def __init__(self, n):
        self.chips = n // 2
        self.half = self.chips // 2
        self.me = lax.axis_index("sp")
        self.z = self.me // 2
        self.c = self.me % 2
        self.right = self.at(1)
        self.left = self.at(-1)
        self.part = self.z * 2 + 1 - self.c

    def at(self, d, other=False):
        c = 1 - self.c if other else self.c
        return lax.rem(self.z + self.chips + d, self.chips) * 2 + c

    def barrier(self):
        bar = pltpu.get_barrier_semaphore()
        for dev in (self.right, self.left, self.part):
            pl.semaphore_signal(bar, inc=1, device_id={"sp": dev}, device_id_type=MESH)
        pl.semaphore_wait(bar, 3)


def remote(src, dst, ss, rs, dev):
    return pltpu.make_async_remote_copy(src_ref=src, dst_ref=dst, send_sem=ss, recv_sem=rs, device_id={"sp": dev}, device_id_type=MESH)


def gather_project(n, pieces, x, wq, wk, wv, inv, meta, xf, qo, ko, vo, mo, xs, wb, qs, ks, vs, ms, tb, cws, cwr, ccs, ccr, pts, ptr, wsem, osem):
    r = Ring(n)
    me, half = r.me, r.half
    sd, hid = x.shape
    rows = sd // pieces
    cols = pl.ds(pl.multiple_of(me * HEAD, HEAD), HEAD)
    own = [pltpu.make_async_copy(w.at[:, cols], wb.at[:, pl.ds(i * HEAD, HEAD)], wsem.at[i]) for i, w in enumerate((wq, wk, wv))]
    own.append(pltpu.make_async_copy(x, xs.at[me], wsem.at[3]))
    own.append(pltpu.make_async_copy(meta, ms.at[me], wsem.at[4]))
    for cp in own:
        cp.start()
    r.barrier()

    def blk(chunk, p):
        return ms.at[chunk] if p == pieces else xs.at[chunk, pl.ds(p * rows, rows)]

    def src(p):
        return meta if p == pieces else x.at[pl.ds(p * rows, rows)]

    sent = []

    def go(cp):
        cp.start()
        sent.append(cp)

    order = [pieces] + list(range(pieces))

    def takes(d, p, cw):
        if d < half:
            return True
        return d == half and (cw if p == pieces else (p < pieces // 2) == cw)

    for p in order:
        go(remote(src(p), blk(me, p), cws.at[0, p], cwr.at[0, p], r.right))
        go(remote(src(p), blk(me, p), ccs.at[0, p], ccr.at[0, p], r.left))
        go(remote(src(p), blk(me, p), pts.at[0, p], ptr.at[0, p], r.part))

    outs = []

    def out(src_, dst, i, slot):
        cp = pltpu.make_async_copy(src_, dst, osem.at[i, slot])
        cp.start()
        outs.append(cp)

    def table(chunk):
        pos = (chunk * sd + lax.broadcasted_iota(jnp.int32, (sd, HEAD), 0)).astype(jnp.float32)
        ang = pos * inv[...]
        si = jnp.sin(ang)
        return jnp.cos(ang), jnp.where(lax.broadcasted_iota(jnp.int32, (sd, HEAD), 1) < HEAD // 2, -si, si)

    def project(chunk, slot, rot=None):
        out(xs.at[chunk], xf.at[chunk], 0, slot)
        acc = jnp.dot(xs[chunk], wb[...], preferred_element_type=jnp.float32)
        co, si = table(chunk) if rot is None else (tb[rot, 0], tb[rot, 1])
        q = acc[:, :HEAD]
        k = acc[:, HEAD : 2 * HEAD]
        qs[chunk] = (q * co + pltpu.roll(q, HEAD // 2, 1) * si).astype(jnp.bfloat16)
        ks[chunk] = (k * co + pltpu.roll(k, HEAD // 2, 1) * si).astype(jnp.bfloat16)
        vs[chunk] = acc[:, 2 * HEAD :].T.astype(jnp.bfloat16)
        out(qs.at[chunk], qo.at[chunk], 1, slot)
        out(ks.at[chunk], ko.at[chunk], 2, slot)
        out(vs.at[chunk], vo.at[:, pl.ds(pl.multiple_of(chunk * sd, sd), sd)], 3, slot)

    def crossed(chunk, s):
        for p in order:
            remote(blk(chunk, p), blk(chunk, p), pts.at[s, p], ptr.at[s, p], r.part).wait_recv()

    for cp in own:
        cp.wait()
    project(me, 0)
    crossed(r.part, 0)
    project(r.part, 1)
    slot = 2
    for d in range(1, half + 1):
        a, b = r.at(-d), r.at(d)
        ao, bo = r.at(-d, True), r.at(d, True)
        s1 = 2 * d - 1
        s2 = 2 * d if d < half else s1
        if d == half:
            for i, chunk in enumerate((a, ao)):
                tb[i, 0], tb[i, 1] = table(chunk)
        for p in order:
            if takes(d, p, True):
                remote(blk(a, p), blk(a, p), cws.at[d - 1, p], cwr.at[d - 1, p], r.right).wait_recv()
                if takes(d + 1, p, True):
                    go(remote(blk(a, p), blk(a, p), cws.at[d, p], cwr.at[d, p], r.right))
                go(remote(blk(a, p), blk(a, p), pts.at[s1, p], ptr.at[s1, p], r.part))
            if takes(d, p, False):
                remote(blk(b, p), blk(b, p), ccs.at[d - 1, p], ccr.at[d - 1, p], r.left).wait_recv()
                if takes(d + 1, p, False):
                    go(remote(blk(b, p), blk(b, p), ccs.at[d, p], ccr.at[d, p], r.left))
                go(remote(blk(b, p), blk(b, p), pts.at[s2, p], ptr.at[s2, p], r.part))
        end = d == half
        project(a, slot, 0 if end else None)
        if not end:
            project(b, slot + 1)
        crossed(ao, s1)
        project(ao, slot + 2 - end, 1 if end else None)
        if not end:
            crossed(bo, s2)
            project(bo, slot + 3)
        slot += 4
    last = pltpu.make_async_copy(ms, mo, wsem.at[5])
    last.start()
    for cp in sent:
        cp.wait_send()
    for cp in outs:
        cp.wait()
    last.wait()


def call_gather_project(x, wq, wk, wv, inv, meta, n, pieces=4):
    sd, hid = x.shape
    half = n // 4
    bf = jnp.bfloat16
    head = jax.ShapeDtypeStruct((n, sd, HEAD), bf)
    return pl.pallas_call(
        functools.partial(gather_project, n, pieces),
        out_shape=(jax.ShapeDtypeStruct((n, sd, hid), bf), head, head, jax.ShapeDtypeStruct((HEAD, n * sd), bf), jax.ShapeDtypeStruct((n,) + meta.shape, meta.dtype)),
        in_specs=[ANY, ANY, ANY, ANY, VM, ANY],
        out_specs=(ANY,) * 5,
        scratch_shapes=[
            pltpu.VMEM((n, sd, hid), bf),
            pltpu.VMEM((hid, 3 * HEAD), bf),
            pltpu.VMEM((n, sd, HEAD), bf),
            pltpu.VMEM((n, sd, HEAD), bf),
            pltpu.VMEM((n, HEAD, sd), bf),
            pltpu.VMEM((n,) + meta.shape, meta.dtype),
            pltpu.VMEM((2, 2, sd, HEAD), jnp.float32),
        ]
        + [DMA((half, pieces + 1))] * 4
        + [DMA((2 * half, pieces + 1))] * 2
        + [DMA((6,)), DMA((4, n))],
        compiler_params=pltpu.CompilerParams(collective_id=1, has_side_effects=True, vmem_limit_bytes=VMEM_BYTES),
        name="gather_project",
    )(x, wq, wk, wv, inv, meta)


def attend_block(i, qT, kb, vT, m, l, acc, sa, sb, between):
    size = qT.shape[1]
    c = math.log2(math.e) / math.sqrt(HEAD)
    m[...] = jnp.full(m.shape, -jnp.inf, jnp.float32)
    l[...] = jnp.zeros(l.shape, jnp.float32)
    acc[...] = jnp.zeros(acc.shape, jnp.float32)

    def at(j):
        return pl.ds(pl.multiple_of(j * size, size), size)

    def score(j, ref):
        ref[...] = jnp.dot(kb[at(j), :], qT[...], preferred_element_type=jnp.float32)

    def soften(j, ref, masked):
        s = ref[...]
        if masked:
            kp = lax.broadcasted_iota(jnp.int32, (size, size), 0)
            qp = lax.broadcasted_iota(jnp.int32, (size, size), 1)
            s = jnp.where(kp <= qp, s, -jnp.inf)
        old = m[...]
        new = jnp.maximum(old, jnp.max(s, axis=0, keepdims=True))
        p = jnp.exp2(s * c - new * c)
        alpha = jnp.exp2((old - new) * c)
        l[...] = l[...] * alpha + jnp.sum(p, axis=0, keepdims=True)
        acc[...] = acc[...] * alpha + jnp.dot(vT[:, at(j)], p.astype(jnp.bfloat16), preferred_element_type=jnp.float32)
        m[...] = new

    score(0, sa)
    between()

    def body(jj, carry):
        score(2 * jj + 1, sb)
        soften(2 * jj, sa, False)
        score(2 * jj + 2, sa)
        soften(2 * jj + 1, sb, False)
        return carry

    lax.fori_loop(0, i // 2, body, 0)

    @pl.when(i % 2 == 1)
    def _():
        score(i, sb)
        soften(i - 1, sa, False)
        soften(i, sb, True)

    @pl.when(i % 2 == 0)
    def _():
        soften(i, sa, True)

    return (acc[...] / l[...]).T.astype(jnp.bfloat16)


def attend_gather(n, q, k, v, xf, wo, hf, o, wb, qb, kb, vb, xb, hb, qT, m, l, acc, sa, sb, cws, cwr, ccs, ccr, pts, ptr, gs, gr, lsem, xsem, hsem):
    r = Ring(n)
    me, half = r.me, r.half
    nb, _, bq, _ = o.shape
    hid = wo.shape[1]
    cut = bq // 2
    tile = 512
    load = [pltpu.make_async_copy(a, b, lsem.at[i]) for i, (a, b) in enumerate(((q, qb), (k, kb), (v, vb), (wo, wb)))]
    for cp in load:
        cp.start()
    pltpu.make_async_copy(xf.at[r.c], xb.at[0], xsem.at[0]).start()
    r.barrier()
    for cp in load[:3]:
        cp.wait()

    lo, hi, whole = pl.ds(0, cut), pl.ds(cut, cut), pl.ds(0, bq)

    def cw(b, d):
        chunk = r.at(-d)
        ref = o.at[b, chunk, lo if d + 1 == half else whole]
        return remote(ref, ref, cws.at[d, b], cwr.at[d, b], r.right)

    def ccw(b, d):
        chunk = r.at(d)
        ref = o.at[b, chunk, hi if d + 1 == half else whole]
        return remote(ref, ref, ccs.at[d, b], ccr.at[d, b], r.left)

    def cw_in(b, d):
        ref = o.at[b, r.at(-d), lo if d == half else whole]
        return remote(ref, ref, cws.at[d - 1, b], cwr.at[d - 1, b], r.right)

    def ccw_in(b, d):
        ref = o.at[b, r.at(d), hi if d == half else whole]
        return remote(ref, ref, ccs.at[d - 1, b], ccr.at[d - 1, b], r.left)

    def cross(b, s, other):
        d = (s + 1) // 2
        sign = -1 if s % 2 == 1 else 1
        rows = whole if d < half else (lo if sign < 0 else hi)
        ref = o.at[b, r.at(sign * d, other), rows]
        return remote(ref, ref, pts.at[s, b], ptr.at[s, b], r.part)

    def mine(b):
        return b % 2 == r.c

    def give(b, s):
        pl.when(b % 2 != r.c)(lambda: cross(b, s, False).start())

    def send(b):
        cw(b, 0).start()
        ccw(b, 0).start()
        give(b, 0)

    def serve(b, d):
        cw_in(b, d).wait_recv()
        if d < half:
            cw(b, d).start()
        give(b, 2 * d - 1)
        ccw_in(b, d).wait_recv()
        if d < half:
            ccw(b, d).start()
        give(b, 2 * d)

    pairs = nb // 2
    ahead = 2
    last = 2 * half - 3

    def attend(i, carry):
        qT[...] = qb[pl.ds(pl.multiple_of(i * 2 * bq, 2 * bq), 2 * bq), :].T

        def between():
            @pl.when(i > 0)
            def _():
                send(2 * i - 2)
                send(2 * i - 1)

            @pl.when(i == pairs - 1)
            def _():
                for b in range(ahead):
                    serve(b, 1)

        out = attend_block(i, qT, kb, vb, m, l, acc, sa, sb, between)
        o[2 * i, me] = out[:bq]
        o[2 * i + 1, me] = out[bq:]
        return carry

    def store(b):
        i = b // 2 % 2
        return pltpu.make_async_copy(hb.at[i], hf.at[b], hsem.at[i])

    def share(b):
        i = b // 2 % 2
        return remote(hb.at[i], hf.at[b], gs.at[b // 2], gr.at[b // 2], r.part)

    def fetch(b):
        i = b // 2 % 2
        return pltpu.make_async_copy(xf.at[b], xb.at[i], xsem.at[i])

    def project(b):
        i = b // 2 % 2
        pl.when(b + 2 < nb)(lambda: fetch(b + 2).start())
        fetch(b).wait()

        @pl.when(b >= 4)
        def _():
            store(b - 4).wait()
            share(b - 4).wait_send()

        def cols(t, carry):
            at = pl.ds(pl.multiple_of(t * tile, tile), tile)
            lhs = jnp.concatenate([o[b, j] for j in range(n)], axis=1)
            y = jnp.dot(lhs, wb[:, at], preferred_element_type=jnp.float32)
            hb[i, :, at] = (xb[i, :, at].astype(jnp.float32) + y).astype(jnp.bfloat16)
            return carry

        lax.fori_loop(0, hid // tile, cols, 0)
        store(b).start()
        share(b).start()

    lax.fori_loop(0, pairs, attend, 0)
    load[3].wait()
    send(nb - 2)
    send(nb - 1)

    def when_in(b, f):
        pl.when(jnp.logical_and(b >= 0, b < nb))(f)

    def step(i, carry):
        for d in range(2, half):
            when_in(i + 4 - 2 * d, lambda d=d: serve(i + 4 - 2 * d, d))
        when_in(i + ahead, lambda: serve(i + ahead, 1))
        when_in(i - last + 1, lambda: serve(i - last + 1, half))
        b = i - last

        @pl.when(jnp.logical_and(b >= 0, mine(b)))
        def _():
            for s in range(2 * half + 1):
                cross(b, s, True).wait_recv()
            project(b)

        return carry

    lax.fori_loop(0, nb + last, step, 0)

    def drain(b, carry):
        for d in range(half):
            cw(b, d).wait_send()
            ccw(b, d).wait_send()

        @pl.when(mine(b))
        def _():
            pl.when(b >= nb - 4)(lambda: (store(b).wait(), share(b).wait_send()) and None)

        @pl.when(jnp.logical_not(mine(b)))
        def _():
            for s in range(2 * half + 1):
                cross(b, s, False).wait_send()
            share(b).wait_recv()

        return carry

    lax.fori_loop(0, nb, drain, 0)


def call_attend_gather(q, k, v, xf, wo, n):
    nb, sd, hid = xf.shape
    half = n // 4
    s = nb * sd
    bf, f32 = jnp.bfloat16, jnp.float32
    return pl.pallas_call(
        functools.partial(attend_gather, n),
        out_shape=jax.ShapeDtypeStruct((nb, sd, hid), bf),
        in_specs=[ANY] * 5,
        out_specs=ANY,
        scratch_shapes=[
            pltpu.VMEM((nb, n, sd, HEAD), bf),
            pltpu.VMEM(wo.shape, bf),
            pltpu.VMEM((s, HEAD), bf),
            pltpu.VMEM((s, HEAD), bf),
            pltpu.VMEM((HEAD, s), bf),
            pltpu.VMEM((2, sd, hid), bf),
            pltpu.VMEM((2, sd, hid), bf),
            pltpu.VMEM((HEAD, 2 * sd), bf),
            pltpu.VMEM((1, 2 * sd), f32),
            pltpu.VMEM((1, 2 * sd), f32),
            pltpu.VMEM((HEAD, 2 * sd), f32),
            pltpu.VMEM((2 * sd, 2 * sd), f32),
            pltpu.VMEM((2 * sd, 2 * sd), f32),
        ]
        + [DMA((half, nb))] * 4
        + [DMA((2 * half + 1, nb))] * 2
        + [DMA((nb // 2,))] * 2
        + [DMA((4,)), DMA((2,)), DMA((2,))],
        compiler_params=pltpu.CompilerParams(collective_id=2, has_side_effects=True, vmem_limit_bytes=VMEM_BYTES),
        name="attend_gather",
    )(q, k, v, xf, wo)


def dispatch(cap, per, meta, hf, h_own, buf, low):
    s = pl.program_id(0)
    me = lax.axis_index("sp")
    group, sd, hid = hf.shape
    kp = meta.shape[1] // 2

    @pl.when(s == 0)
    def _():
        earlier = lax.broadcasted_iota(jnp.int32, (sd, sd), 0) < lax.broadcasted_iota(jnp.int32, (sd, sd), 1)
        low[...] = jnp.where(earlier, 1.0, 0.0).astype(jnp.bfloat16)

    mine, gate = [], []
    for i in range(group):
        chosen, gates = meta[i, :kp, :], meta[i, kp:, :]
        for j in range(per):
            hit = chosen == (me * per + j).astype(jnp.float32)
            mine.append(jnp.max(jnp.where(hit, 1.0, 0.0), axis=0, keepdims=True))
            gate.append(jnp.sum(jnp.where(hit, gates, 0.0), axis=0, keepdims=True))
    every = jnp.concatenate(mine, axis=0)
    rank = jnp.dot(every.astype(jnp.bfloat16), low[...], preferred_element_type=jnp.float32)
    rank = jnp.where(every > 0.5, rank, -1.0)
    place = lax.broadcasted_iota(jnp.int32, (cap, sd), 0).astype(jnp.float32)
    tile = 512
    pick, w = [], []
    for i in range(group):
        picks, ws = [], []
        for j in range(per):
            at = rank[i * per + j : i * per + j + 1, :] == place
            picks.append(jnp.where(at, 1.0, 0.0))
            ws.append(jnp.sum(jnp.where(at, gate[i * per + j], 0.0), axis=1, keepdims=True))
        pick.append(jnp.concatenate(picks, axis=0).astype(jnp.bfloat16))
        w.append(jnp.concatenate(ws, axis=0))
    for t in range(hid // tile):
        cols = pl.ds(t * tile, tile)
        rows = [w[i] * jnp.dot(pick[i], hf[i, :, cols], preferred_element_type=jnp.float32) for i in range(group)]
        for j in range(per):
            buf[j, :, cols] = jnp.concatenate([y[j * cap : (j + 1) * cap] for y in rows], axis=0).astype(jnp.bfloat16)

    @pl.when(s == me // group)
    def _():
        h_own[...] = hf[me % group]


def call_dispatch(meta, hf, cap, per, group=2):
    n, sd, hid = hf.shape
    return pl.pallas_call(
        functools.partial(dispatch, cap, per),
        grid=(n // group,),
        out_shape=(jax.ShapeDtypeStruct((sd, hid), jnp.bfloat16), jax.ShapeDtypeStruct((per, n * cap, hid), jnp.bfloat16)),
        in_specs=[pl.BlockSpec((group,) + meta.shape[1:], lambda s: (s, 0, 0)), pl.BlockSpec((group, sd, hid), lambda s: (s, 0, 0))],
        out_specs=(pl.BlockSpec((sd, hid), lambda s: (0, 0)), pl.BlockSpec((per, group * cap, hid), lambda s: (0, s, 0))),
        scratch_shapes=[pltpu.VMEM((sd, sd), jnp.bfloat16)],
        compiler_params=pltpu.CompilerParams(dimension_semantics=("arbitrary",), vmem_limit_bytes=48 * 1024 * 1024),
        name="dispatch",
    )(meta, hf)


def routing(idx, probs):
    top = idx.shape[1]
    pad = -top % 8
    hot = idx[:, :, None] == jnp.arange(probs.shape[1])[None, None, :]
    sel = jnp.sum(jnp.where(hot, probs[:, None, :], 0.0), axis=2)
    w = sel / jnp.sum(sel, axis=1, keepdims=True)
    e = jnp.pad(idx.astype(jnp.float32), ((0, 0), (0, pad)), constant_values=-1.0)
    return jnp.concatenate([e, jnp.pad(w, ((0, 0), (0, pad)))], axis=1).T


def solution(mesh):
    n = mesh.shape["sp"]
    row = P(("dp", "sp"), None)
    full = P(None, None)

    def local(x, wq, wk, wv, wo, idx, probs):
        sd, hid = x.shape
        ne = probs.shape[1]
        cap = 2 * sd * idx.shape[1] // ne
        inv = ROPE_BASE ** (-jnp.arange(HEAD // 2, dtype=jnp.float32) * (2.0 / HEAD))
        inv = jnp.concatenate([inv, inv])[None, :]
        meta = routing(idx, probs)
        xf, q, k, v, metas = call_gather_project(x, wq, wk, wv, inv, meta, n)
        q, k = (a.reshape(n * sd, HEAD) for a in (q, k))
        hf = call_attend_gather(q, k, v, xf, wo, n)
        h, buf = call_dispatch(metas, hf, cap, ne // n)
        return h, buf

    return jax.shard_map(local, mesh=mesh, in_specs=(row, full, full, full, full, row, row), out_specs=(row, P(("dp", "sp"), None, None)), check_vma=False)
```

time: 368 us -> 305 us (0.83)
  Pallas kernels: 361 us -> 300 us
    pallas_call x1, Pallas kernels: 196 us -> 141 us  [call_attend_gather(): pl.pallas_call(functools.partial(attend_gather, n), out_shape=jax.ShapeDt...]
    pallas_call x1, Pallas kernels: 25.4 us -> 21.4 us  [call_dispatch(): pl.pallas_call(functools.partial(dispatch, cap, per), grid=(n // group,),...]
where the time goes in v2:
time: 305 us; the launch traced here: 304 us
  Pallas kernels  300 us (98%)
    pallas_call x1, Pallas kernels, call_attend_gather(): pl.pallas_call(functools.partial(attend_gather, n), out_shape=jax.ShapeDt...  141 us
    pallas_call x1, Pallas kernels, call_gather_project(): pl.pallas_call(functools.partial(gather_project, n, pieces), out_shape=(j...  138 us
    pallas_call x1, Pallas kernels, call_dispatch(): pl.pallas_call(functools.partial(dispatch, cap, per), grid=(n // group,),...  21.4 us

profile of v2, /device:TPU:21, one launch (start us, length us, event | category | flops | bytes accessed | tf_op | source)
XLA Modules:
  0.0 304.4 jit_solution(9308500160894392303)
XLA Ops:
  0.6 0.6 maximum_bitcast_fusion.inv
  1.2 0.7 convert_element_type.5
  1.9 1.0 select_reduce_fusion
  3.0 0.6 fusion.meta
  3.6 137.6 %gather_project.1 = (bf16[16,384,2048]{2,1,0:T(8,128)(2,1)}, bf16[16,384,128]{2,1,0:T(8,128)(2,1)}, bf16[16,384,128]{2,1,0:T(8,128)(2,1)}, bf16[128,6144]{1,0:T(8,128)(2,1)}, f32[16,16,384]{2,1,0:T(8,128)}) custom-call(bf16[384,2048]{1,0:T(8,128)(2,1)} %x.5, bf16[2048,2048]{1,0:T(8,128)(2,1)} %wq.1, bf16[2048,2048]{1,0:T(8,128)(2,1)} %wk.1, ...), custom_call_target="tpu_custom_call" | custom-call | tf_op jit(solution)/shard_map/gather_project/pallas_call | solution.py:161
  141.2 140.8 %attend_gather.1.hf = bf16[16,384,2048]{2,1,0:T(8,128)(2,1)} custom-call(bf16[6144,128]{1,0:T(8,128)(2,1)} %bitcast.6, bf16[6144,128]{1,0:T(8,128)(2,1)} %bitcast.7, bf16[128,6144]{1,0:T(8,128)(2,1)} %get-tuple-element.10.v, bf16[16,384,2048]{2,1,0:T(8,128)(2,1)} %get-tuple-element.11.xf, bf16[2048,2048]{1,0:T(8,128)(2,1)} %wo.1), custom_call_target="tpu_custom_call" | custom-call | tf_op jit(solution)/shard_map/attend_gather/pallas_call | solution.py:404
  282.0 0.0 copy-start
  282.0 1.0 copy-done
  283.0 21.4 %dispatch.1 = (bf16[384,2048]{1,0:T(8,128)(2,1)}, bf16[4,1152,2048]{2,1,0:T(8,128)(2,1)}) custom-call(f32[16,16,384]{2,1,0:T(8,128)S(1)} %copy-done, bf16[16,384,2048]{2,1,0:T(8,128)(2,1)} %attend_gather.1.hf), custom_call_target="tpu_custom_call" | custom-call | tf_op jit(solution)/shard_map/dispatch/pallas_call | solution.py:478
  (2 shorter events, 0.0 us)
Async XLA Ops:
  282.0 1.0 copy-start

commit v3 on v2

--- a/solution.py
+++ b/solution.py
@@ -2,6 +2,7 @@
 import math
 import jax
 import jax.numpy as jnp
+import numpy as np
 from jax import lax
 from jax.experimental import pallas as pl
 from jax.experimental.pallas import tpu as pltpu
@@ -238,11 +239,14 @@
     nb, _, bq, _ = o.shape
     hid = wo.shape[1]
     cut = bq // 2
+    width = hid // 2
     tile = 512
-    load = [pltpu.make_async_copy(a, b, lsem.at[i]) for i, (a, b) in enumerate(((q, qb), (k, kb), (v, vb), (wo, wb)))]
+    tiles = width // tile
+    half_cols = pl.ds(pl.multiple_of(r.c * width, width), width)
+    load = [pltpu.make_async_copy(a, b, lsem.at[i]) for i, (a, b) in enumerate(((q, qb), (k, kb), (v, vb), (wo.at[:, half_cols], wb)))]
     for cp in load:
         cp.start()
-    pltpu.make_async_copy(xf.at[r.c], xb.at[0], xsem.at[0]).start()
+    pltpu.make_async_copy(xf.at[0, :, half_cols], xb.at[0], xsem.at[0]).start()
     r.barrier()
     for cp in load[:3]:
         cp.wait()
@@ -274,11 +278,8 @@
         ref = o.at[b, r.at(sign * d, other), rows]
         return remote(ref, ref, pts.at[s, b], ptr.at[s, b], r.part)
 
-    def mine(b):
-        return b % 2 == r.c
-
     def give(b, s):
-        pl.when(b % 2 != r.c)(lambda: cross(b, s, False).start())
+        cross(b, s, False).start()
 
     def send(b):
         cw(b, 0).start()
@@ -319,37 +320,36 @@
         return carry
 
     def store(b):
-        i = b // 2 % 2
-        return pltpu.make_async_copy(hb.at[i], hf.at[b], hsem.at[i])
-
-    def share(b):
-        i = b // 2 % 2
-        return remote(hb.at[i], hf.at[b], gs.at[b // 2], gr.at[b // 2], r.part)
+        return pltpu.make_async_copy(hb.at[b % 2], hf.at[b, :, half_cols], hsem.at[b % 2])
+
+    def share(b, t):
+        to = pl.ds(pl.multiple_of(r.c * width + t * tile, tile), tile)
+        return remote(hb.at[b % 2, :, pl.ds(pl.multiple_of(t * tile, tile), tile)], hf.at[b, :, to], gs.at[b, t], gr.at[b, t], r.part)
 
     def fetch(b):
-        i = b // 2 % 2
-        return pltpu.make_async_copy(xf.at[b], xb.at[i], xsem.at[i])
+        return pltpu.make_async_copy(xf.at[b, :, half_cols], xb.at[b % 2], xsem.at[b % 2])
 
     def project(b):
-        i = b // 2 % 2
-        pl.when(b + 2 < nb)(lambda: fetch(b + 2).start())
+        i = b % 2
+        pl.when(b + 1 < nb)(lambda: fetch(b + 1).start())
         fetch(b).wait()
 
-        @pl.when(b >= 4)
+        @pl.when(b >= 2)
         def _():
-            store(b - 4).wait()
-            share(b - 4).wait_send()
+            store(b - 2).wait()
+            for t in range(tiles):
+                share(b - 2, t).wait_send()
 
         def cols(t, carry):
             at = pl.ds(pl.multiple_of(t * tile, tile), tile)
             lhs = jnp.concatenate([o[b, j] for j in range(n)], axis=1)
             y = jnp.dot(lhs, wb[:, at], preferred_element_type=jnp.float32)
             hb[i, :, at] = (xb[i, :, at].astype(jnp.float32) + y).astype(jnp.bfloat16)
+            share(b, t).start()
             return carry
 
-        lax.fori_loop(0, hid // tile, cols, 0)
+        lax.fori_loop(0, tiles, cols, 0)
         store(b).start()
-        share(b).start()
 
     lax.fori_loop(0, pairs, attend, 0)
     load[3].wait()
@@ -366,7 +366,7 @@
         when_in(i - last + 1, lambda: serve(i - last + 1, half))
         b = i - last
 
-        @pl.when(jnp.logical_and(b >= 0, mine(b)))
+        @pl.when(b >= 0)
         def _():
             for s in range(2 * half + 1):
                 cross(b, s, True).wait_recv()
@@ -381,15 +381,16 @@
             cw(b, d).wait_send()
             ccw(b, d).wait_send()
 
-        @pl.when(mine(b))
+        for s in range(2 * half + 1):
+            cross(b, s, False).wait_send()
+        for t in range(tiles):
+            share(b, t).wait_recv()
+
+        @pl.when(b >= nb - 2)
         def _():
-            pl.when(b >= nb - 4)(lambda: (store(b).wait(), share(b).wait_send()) and None)
-
-        @pl.when(jnp.logical_not(mine(b)))
-        def _():
-            for s in range(2 * half + 1):
-                cross(b, s, False).wait_send()
-            share(b).wait_recv()
+            store(b).wait()
+            for t in range(tiles):
+                share(b, t).wait_send()
 
         return carry
 
@@ -408,12 +409,12 @@
         out_specs=ANY,
         scratch_shapes=[
             pltpu.VMEM((nb, n, sd, HEAD), bf),
-            pltpu.VMEM(wo.shape, bf),
+            pltpu.VMEM((wo.shape[0], hid // 2), bf),
             pltpu.VMEM((s, HEAD), bf),
             pltpu.VMEM((s, HEAD), bf),
             pltpu.VMEM((HEAD, s), bf),
-            pltpu.VMEM((2, sd, hid), bf),
-            pltpu.VMEM((2, sd, hid), bf),
+            pltpu.VMEM((2, sd, hid // 2), bf),
+            pltpu.VMEM((2, sd, hid // 2), bf),
             pltpu.VMEM((HEAD, 2 * sd), bf),
             pltpu.VMEM((1, 2 * sd), f32),
             pltpu.VMEM((1, 2 * sd), f32),
@@ -423,66 +424,90 @@
         ]
         + [DMA((half, nb))] * 4
         + [DMA((2 * half + 1, nb))] * 2
-        + [DMA((nb // 2,))] * 2
+        + [DMA((nb, hid // 1024))] * 2
         + [DMA((4,)), DMA((2,)), DMA((2,))],
         compiler_params=pltpu.CompilerParams(collective_id=2, has_side_effects=True, vmem_limit_bytes=VMEM_BYTES),
         name="attend_gather",
     )(q, k, v, xf, wo)
 
 
-def dispatch(cap, per, meta, hf, h_own, buf, low):
-    s = pl.program_id(0)
+def dispatch(cap, per, meta, hf, h_own, buf, hv, bv, low, isem, osem, hsem):
     me = lax.axis_index("sp")
-    group, sd, hid = hf.shape
+    n, sd, hid = hf.shape
     kp = meta.shape[1] // 2
-
-    @pl.when(s == 0)
-    def _():
-        earlier = lax.broadcasted_iota(jnp.int32, (sd, sd), 0) < lax.broadcasted_iota(jnp.int32, (sd, sd), 1)
-        low[...] = jnp.where(earlier, 1.0, 0.0).astype(jnp.bfloat16)
-
-    mine, gate = [], []
-    for i in range(group):
-        chosen, gates = meta[i, :kp, :], meta[i, kp:, :]
+    tile = 512
+
+    def fetch(s):
+        return pltpu.make_async_copy(hf.at[s], hv.at[s], isem.at[s])
+
+    def store(s, j):
+        return pltpu.make_async_copy(bv.at[s, j], buf.at[j, pl.ds(pl.multiple_of(s * cap, 8), cap)], osem.at[s, j])
+
+    for s in range(n):
+        fetch(s).start()
+    earlier = lax.broadcasted_iota(jnp.int32, (sd, sd), 0) < lax.broadcasted_iota(jnp.int32, (sd, sd), 1)
+    low[...] = jnp.where(earlier, 1.0, 0.0).astype(jnp.bfloat16)
+    place = lax.broadcasted_iota(jnp.int32, (cap, sd), 0).astype(jnp.float32)
+
+    def source(s, carry):
+        chosen, gates = meta[s, :kp, :], meta[s, kp:, :]
+        mine, gate = [], []
         for j in range(per):
             hit = chosen == (me * per + j).astype(jnp.float32)
             mine.append(jnp.max(jnp.where(hit, 1.0, 0.0), axis=0, keepdims=True))
             gate.append(jnp.sum(jnp.where(hit, gates, 0.0), axis=0, keepdims=True))
-    every = jnp.concatenate(mine, axis=0)
-    rank = jnp.dot(every.astype(jnp.bfloat16), low[...], preferred_element_type=jnp.float32)
-    rank = jnp.where(every > 0.5, rank, -1.0)
-    place = lax.broadcasted_iota(jnp.int32, (cap, sd), 0).astype(jnp.float32)
-    tile = 512
-    pick, w = [], []
-    for i in range(group):
+        every = jnp.concatenate(mine + [jnp.zeros((8 - per, sd), jnp.float32)], axis=0)
+        rank = jnp.dot(every.astype(jnp.bfloat16), low[...], preferred_element_type=jnp.float32)
+        rank = jnp.where(every > 0.5, rank, -1.0)
         picks, ws = [], []
         for j in range(per):
-            at = rank[i * per + j : i * per + j + 1, :] == place
+            at = rank[j : j + 1, :] == place
             picks.append(jnp.where(at, 1.0, 0.0))
-            ws.append(jnp.sum(jnp.where(at, gate[i * per + j], 0.0), axis=1, keepdims=True))
-        pick.append(jnp.concatenate(picks, axis=0).astype(jnp.bfloat16))
-        w.append(jnp.concatenate(ws, axis=0))
-    for t in range(hid // tile):
-        cols = pl.ds(t * tile, tile)
-        rows = [w[i] * jnp.dot(pick[i], hf[i, :, cols], preferred_element_type=jnp.float32) for i in range(group)]
+            ws.append(jnp.sum(jnp.where(at, gate[j], 0.0), axis=1, keepdims=True))
+        pick = jnp.concatenate(picks, axis=0).astype(jnp.bfloat16)
+        w = jnp.concatenate(ws, axis=0)
+        fetch(s).wait()
+        for t in range(hid // tile):
+            cols = pl.ds(t * tile, tile)
+            rows = w * jnp.dot(pick, hv[s, :, cols], preferred_element_type=jnp.float32)
+            for j in range(per):
+                bv[s, j, :, cols] = rows[j * cap : (j + 1) * cap, :].astype(jnp.bfloat16)
         for j in range(per):
-            buf[j, :, cols] = jnp.concatenate([y[j * cap : (j + 1) * cap] for y in rows], axis=0).astype(jnp.bfloat16)
-
-    @pl.when(s == me // group)
-    def _():
-        h_own[...] = hf[me % group]
-
-
-def call_dispatch(meta, hf, cap, per, group=2):
+            store(s, j).start()
+
+        @pl.when(s == me)
+        def _():
+            pltpu.make_async_copy(hv.at[s], h_own, hsem).start()
+
+        return carry
+
+    lax.fori_loop(0, n, source, 0)
+
+    def drain(s, carry):
+        for j in range(per):
+            store(s, j).wait()
+        return carry
+
+    lax.fori_loop(0, n, drain, 0)
+    pltpu.make_async_copy(hv.at[me], h_own, hsem).wait()
+
+
+def call_dispatch(meta, hf, cap, per):
     n, sd, hid = hf.shape
     return pl.pallas_call(
         functools.partial(dispatch, cap, per),
-        grid=(n // group,),
         out_shape=(jax.ShapeDtypeStruct((sd, hid), jnp.bfloat16), jax.ShapeDtypeStruct((per, n * cap, hid), jnp.bfloat16)),
-        in_specs=[pl.BlockSpec((group,) + meta.shape[1:], lambda s: (s, 0, 0)), pl.BlockSpec((group, sd, hid), lambda s: (s, 0, 0))],
-        out_specs=(pl.BlockSpec((sd, hid), lambda s: (0, 0)), pl.BlockSpec((per, group * cap, hid), lambda s: (0, s, 0))),
-        scratch_shapes=[pltpu.VMEM((sd, sd), jnp.bfloat16)],
-        compiler_params=pltpu.CompilerParams(dimension_semantics=("arbitrary",), vmem_limit_bytes=48 * 1024 * 1024),
+        in_specs=[VM, ANY],
+        out_specs=(ANY, ANY),
+        scratch_shapes=[
+            pltpu.VMEM((n, sd, hid), jnp.bfloat16),
+            pltpu.VMEM((n, per, cap, hid), jnp.bfloat16),
+            pltpu.VMEM((sd, sd), jnp.bfloat16),
+            DMA((n,)),
+            DMA((n, per)),
+            DMA,
+        ],
+        compiler_params=pltpu.CompilerParams(vmem_limit_bytes=VMEM_BYTES),
         name="dispatch",
     )(meta, hf)
 
@@ -506,8 +531,7 @@
         sd, hid = x.shape
         ne = probs.shape[1]
         cap = 2 * sd * idx.shape[1] // ne
-        inv = ROPE_BASE ** (-jnp.arange(HEAD // 2, dtype=jnp.float32) * (2.0 / HEAD))
-        inv = jnp.concatenate([inv, inv])[None, :]
+        inv = jnp.asarray(np.tile(ROPE_BASE ** (-np.arange(HEAD // 2) * (2.0 / HEAD)), 2)[None, :], jnp.float32)
         meta = routing(idx, probs)
         xf, q, k, v, metas = call_gather_project(x, wq, wk, wv, inv, meta, n)
         q, k = (a.reshape(n * sd, HEAD) for a in (q, k))

time: 305 us -> 299 us (0.980)
  Pallas kernels: 300 us -> 296 us
    pallas_call x1, Pallas kernels: 141 us -> 137 us  [call_attend_gather(): pl.pallas_call(functools.partial(attend_gather, n), out_shape=jax.ShapeDt...]
where the time goes in v3:
time: 299 us
  Pallas kernels  296 us (99%)
    pallas_call x1, Pallas kernels, call_gather_project(): pl.pallas_call(functools.partial(gather_project, n, pieces), out_shape=(j...  138 us
    pallas_call x1, Pallas kernels, call_attend_gather(): pl.pallas_call(functools.partial(attend_gather, n), out_shape=jax.ShapeDt...  137 us
    pallas_call x1, Pallas kernels, call_dispatch(): pl.pallas_call(functools.partial(dispatch, cap, per), out_shape=(jax.Shap...  21.1 us

profile of v3, /device:TPU:21, one launch (start us, length us, event | category | flops | bytes accessed | tf_op | source)
XLA Modules:
  0.0 299.1 jit_solution(17855369620747594646)
XLA Ops:
  0.6 0.7 convert_element_type.5
  1.3 1.0 select_reduce_fusion
  2.4 0.6 fusion.meta
  3.0 137.6 %gather_project.1 = (bf16[16,384,2048]{2,1,0:T(8,128)(2,1)}, bf16[16,384,128]{2,1,0:T(8,128)(2,1)}, bf16[16,384,128]{2,1,0:T(8,128)(2,1)}, bf16[128,6144]{1,0:T(8,128)(2,1)}, f32[16,16,384]{2,1,0:T(8,128)}) custom-call(bf16[384,2048]{1,0:T(8,128)(2,1)} %x.5, bf16[2048,2048]{1,0:T(8,128)(2,1)} %wq.1, bf16[2048,2048]{1,0:T(8,128)(2,1)} %wk.1, ...), custom_call_target="tpu_custom_call" | custom-call | tf_op jit(solution)/shard_map/gather_project/pallas_call | solution.py:162
  140.6 137.3 %attend_gather.1.hf = bf16[16,384,2048]{2,1,0:T(8,128)(2,1)} custom-call(bf16[6144,128]{1,0:T(8,128)(2,1)} %bitcast.4, bf16[6144,128]{1,0:T(8,128)(2,1)} %bitcast.5, bf16[128,6144]{1,0:T(8,128)(2,1)} %get-tuple-element.10.v, bf16[16,384,2048]{2,1,0:T(8,128)(2,1)} %get-tuple-element.11.xf, bf16[2048,2048]{1,0:T(8,128)(2,1)} %wo.1), custom_call_target="tpu_custom_call" | custom-call | tf_op jit(solution)/shard_map/attend_gather/pallas_call | solution.py:405
  277.8 21.1 %dispatch.1 = (bf16[384,2048]{1,0:T(8,128)(2,1)}, bf16[4,1152,2048]{2,1,0:T(8,128)(2,1)}) custom-call(f32[16,16,384]{2,1,0:T(8,128)} %get-tuple-element.7.meta, bf16[16,384,2048]{2,1,0:T(8,128)(2,1)} %attend_gather.1.hf), custom_call_target="tpu_custom_call" | custom-call | tf_op jit(solution)/shard_map/dispatch/pallas_call | solution.py:497
  (1 shorter events, 0.0 us)

commit v4 on v3

--- a/solution.py
+++ b/solution.py
@@ -43,7 +43,18 @@
     return pltpu.make_async_remote_copy(src_ref=src, dst_ref=dst, send_sem=ss, recv_sem=rs, device_id={"sp": dev}, device_id_type=MESH)
 
 
-def gather_project(n, pieces, x, wq, wk, wv, inv, meta, xf, qo, ko, vo, mo, xs, wb, qs, ks, vs, ms, tb, cws, cwr, ccs, ccr, pts, ptr, wsem, osem):
+def routing(idx, probs, half):
+    top, sd = idx.shape
+    expert = lax.broadcasted_iota(jnp.int32, probs.shape, 0)
+    chosen = [idx[c : c + 1, :] for c in range(top)]
+    sel = [jnp.sum(jnp.where(expert == e, probs[...], 0.0), axis=0, keepdims=True) for e in chosen]
+    total = sum(sel[1:], sel[0])
+    rows = [e.astype(jnp.float32) for e in chosen] + [jnp.full((half - top, sd), -1.0, jnp.float32)] * (half > top)
+    rows += [w / total for w in sel] + [jnp.zeros((half - top, sd), jnp.float32)] * (half > top)
+    return jnp.concatenate(rows, axis=0)
+
+
+def gather_project(n, pieces, x, wq, wk, wv, inv, idx, probs, xf, qo, ko, vo, mo, xs, wb, qs, ks, vs, ms, tb, cws, cwr, ccs, ccr, pts, ptr, wsem, osem):
     r = Ring(n)
     me, half = r.me, r.half
     sd, hid = x.shape
@@ -51,7 +62,6 @@
     cols = pl.ds(pl.multiple_of(me * HEAD, HEAD), HEAD)
     own = [pltpu.make_async_copy(w.at[:, cols], wb.at[:, pl.ds(i * HEAD, HEAD)], wsem.at[i]) for i, w in enumerate((wq, wk, wv))]
     own.append(pltpu.make_async_copy(x, xs.at[me], wsem.at[3]))
-    own.append(pltpu.make_async_copy(meta, ms.at[me], wsem.at[4]))
     for cp in own:
         cp.start()
     r.barrier()
@@ -60,7 +70,7 @@
         return ms.at[chunk] if p == pieces else xs.at[chunk, pl.ds(p * rows, rows)]
 
     def src(p):
-        return meta if p == pieces else x.at[pl.ds(p * rows, rows)]
+        return ms.at[me] if p == pieces else x.at[pl.ds(p * rows, rows)]
 
     sent = []
 
@@ -68,17 +78,21 @@
         cp.start()
         sent.append(cp)
 
-    order = [pieces] + list(range(pieces))
+    order = list(range(pieces + 1))
 
     def takes(d, p, cw):
         if d < half:
             return True
         return d == half and (cw if p == pieces else (p < pieces // 2) == cw)
 
-    for p in order:
+    def first(p):
         go(remote(src(p), blk(me, p), cws.at[0, p], cwr.at[0, p], r.right))
         go(remote(src(p), blk(me, p), ccs.at[0, p], ccr.at[0, p], r.left))
         go(remote(src(p), blk(me, p), pts.at[0, p], ptr.at[0, p], r.part))
+
+    for p in range(pieces):
+        first(p)
+    ms[me] = routing(idx, probs, ms.shape[1] // 2)
 
     outs = []
 
@@ -113,6 +127,7 @@
     for cp in own:
         cp.wait()
     project(me, 0)
+    first(pieces)
     crossed(r.part, 0)
     project(r.part, 1)
     slot = 2
@@ -154,15 +169,16 @@
     last.wait()
 
 
-def call_gather_project(x, wq, wk, wv, inv, meta, n, pieces=4):
+def call_gather_project(x, wq, wk, wv, inv, idx, probs, n, pieces=4):
     sd, hid = x.shape
     half = n // 4
     bf = jnp.bfloat16
     head = jax.ShapeDtypeStruct((n, sd, HEAD), bf)
+    meta = jax.ShapeDtypeStruct((n, 2 * (idx.shape[0] + -idx.shape[0] % 8), sd), jnp.float32)
     return pl.pallas_call(
         functools.partial(gather_project, n, pieces),
-        out_shape=(jax.ShapeDtypeStruct((n, sd, hid), bf), head, head, jax.ShapeDtypeStruct((HEAD, n * sd), bf), jax.ShapeDtypeStruct((n,) + meta.shape, meta.dtype)),
-        in_specs=[ANY, ANY, ANY, ANY, VM, ANY],
+        out_shape=(jax.ShapeDtypeStruct((n, sd, hid), bf), head, head, jax.ShapeDtypeStruct((HEAD, n * sd), bf), meta),
+        in_specs=[ANY, ANY, ANY, ANY, VM, VM, VM],
         out_specs=(ANY,) * 5,
         scratch_shapes=[
             pltpu.VMEM((n, sd, hid), bf),
@@ -170,7 +186,7 @@
             pltpu.VMEM((n, sd, HEAD), bf),
             pltpu.VMEM((n, sd, HEAD), bf),
             pltpu.VMEM((n, HEAD, sd), bf),
-            pltpu.VMEM((n,) + meta.shape, meta.dtype),
+            pltpu.VMEM(meta.shape, meta.dtype),
             pltpu.VMEM((2, 2, sd, HEAD), jnp.float32),
         ]
         + [DMA((half, pieces + 1))] * 4
@@ -178,7 +194,7 @@
         + [DMA((6,)), DMA((4, n))],
         compiler_params=pltpu.CompilerParams(collective_id=1, has_side_effects=True, vmem_limit_bytes=VMEM_BYTES),
         name="gather_project",
-    )(x, wq, wk, wv, inv, meta)
+    )(x, wq, wk, wv, inv, idx, probs)
 
 
 def attend_block(i, qT, kb, vT, m, l, acc, sa, sb, between):
@@ -243,7 +259,11 @@
     tile = 512
     tiles = width // tile
     half_cols = pl.ds(pl.multiple_of(r.c * width, width), width)
-    load = [pltpu.make_async_copy(a, b, lsem.at[i]) for i, (a, b) in enumerate(((q, qb), (k, kb), (v, vb), (wo.at[:, half_cols], wb)))]
+    head, tail = pl.ds(0, 2 * bq), pl.ds(2 * bq, (nb - 2) * bq)
+    parts = [(a.at[rows], b.at[rows]) for rows in (head, tail) for a, b in ((q, qb), (k, kb))]
+    parts[2:2] = [(v.at[:, head], vb.at[:, head])]
+    parts += [(v.at[:, tail], vb.at[:, tail]), (wo.at[:, half_cols], wb)]
+    load = [pltpu.make_async_copy(a, b, lsem.at[i]) for i, (a, b) in enumerate(parts)]
     for cp in load:
         cp.start()
     pltpu.make_async_copy(xf.at[0, :, half_cols], xb.at[0], xsem.at[0]).start()
@@ -301,6 +321,11 @@
     last = 2 * half - 3
 
     def attend(i, carry):
+        @pl.when(i == 1)
+        def _():
+            for cp in load[3:6]:
+                cp.wait()
+
         qT[...] = qb[pl.ds(pl.multiple_of(i * 2 * bq, 2 * bq), 2 * bq), :].T
 
         def between():
@@ -352,7 +377,7 @@
         store(b).start()
 
     lax.fori_loop(0, pairs, attend, 0)
-    load[3].wait()
+    load[6].wait()
     send(nb - 2)
     send(nb - 1)
 
@@ -425,7 +450,7 @@
         + [DMA((half, nb))] * 4
         + [DMA((2 * half + 1, nb))] * 2
         + [DMA((nb, hid // 1024))] * 2
-        + [DMA((4,)), DMA((2,)), DMA((2,))],
+        + [DMA((7,)), DMA((2,)), DMA((2,))],
         compiler_params=pltpu.CompilerParams(collective_id=2, has_side_effects=True, vmem_limit_bytes=VMEM_BYTES),
         name="attend_gather",
     )(q, k, v, xf, wo)
@@ -512,16 +537,6 @@
     )(meta, hf)
 
 
-def routing(idx, probs):
-    top = idx.shape[1]
-    pad = -top % 8
-    hot = idx[:, :, None] == jnp.arange(probs.shape[1])[None, None, :]
-    sel = jnp.sum(jnp.where(hot, probs[:, None, :], 0.0), axis=2)
-    w = sel / jnp.sum(sel, axis=1, keepdims=True)
-    e = jnp.pad(idx.astype(jnp.float32), ((0, 0), (0, pad)), constant_values=-1.0)
-    return jnp.concatenate([e, jnp.pad(w, ((0, 0), (0, pad)))], axis=1).T
-
-
 def solution(mesh):
     n = mesh.shape["sp"]
     row = P(("dp", "sp"), None)
@@ -532,8 +547,7 @@
         ne = probs.shape[1]
         cap = 2 * sd * idx.shape[1] // ne
         inv = jnp.asarray(np.tile(ROPE_BASE ** (-np.arange(HEAD // 2) * (2.0 / HEAD)), 2)[None, :], jnp.float32)
-        meta = routing(idx, probs)
-        xf, q, k, v, metas = call_gather_project(x, wq, wk, wv, inv, meta, n)
+        xf, q, k, v, metas = call_gather_project(x, wq, wk, wv, inv, idx.T, probs.T, n)
         q, k = (a.reshape(n * sd, HEAD) for a in (q, k))
         hf = call_attend_gather(q, k, v, xf, wo, n)
         h, buf = call_dispatch(metas, hf, cap, ne // n)

time: 299 us -> 296 us (0.990)
  no operation moved by 1% of the time
where the time goes in v4:
time: 296 us
  Pallas kernels  295 us (100%)
    pallas_call x1, Pallas kernels, call_gather_project(): pl.pallas_call(functools.partial(gather_project, n, pieces), out_shape=(j...  138 us
    pallas_call x1, Pallas kernels, call_attend_gather(): pl.pallas_call(functools.partial(attend_gather, n), out_shape=jax.ShapeDt...  137 us
    pallas_call x1, Pallas kernels, call_dispatch(): pl.pallas_call(functools.partial(dispatch, cap, per), out_shape=(jax.Shap...  21.1 us

profile of v4, /device:TPU:21, one launch (start us, length us, event | category | flops | bytes accessed | tf_op | source)
XLA Modules:
  0.0 296.3 jit_solution(3917675091891885369)
XLA Ops:
  0.6 137.7 %gather_project.1 = (bf16[16,384,2048]{2,1,0:T(8,128)(2,1)}, bf16[16,384,128]{2,1,0:T(8,128)(2,1)}, bf16[16,384,128]{2,1,0:T(8,128)(2,1)}, bf16[128,6144]{1,0:T(8,128)(2,1)}, f32[16,16,384]{2,1,0:T(8,128)}) custom-call(bf16[384,2048]{1,0:T(8,128)(2,1)} %x.1, bf16[2048,2048]{1,0:T(8,128)(2,1)} %wq.1, bf16[2048,2048]{1,0:T(8,128)(2,1)} %wk.1, ...), custom_call_target="tpu_custom_call" | custom-call | tf_op jit(solution)/shard_map/gather_project/pallas_call | solution.py:178
  138.3 136.7 %attend_gather.1.hf = bf16[16,384,2048]{2,1,0:T(8,128)(2,1)} custom-call(bf16[6144,128]{1,0:T(8,128)(2,1)} %bitcast.4, bf16[6144,128]{1,0:T(8,128)(2,1)} %bitcast.5, bf16[128,6144]{1,0:T(8,128)(2,1)} %get-tuple-element.10.v, bf16[16,384,2048]{2,1,0:T(8,128)(2,1)} %get-tuple-element.11.xf, bf16[2048,2048]{1,0:T(8,128)(2,1)} %wo.1), custom_call_target="tpu_custom_call" | custom-call | tf_op jit(solution)/shard_map/attend_gather/pallas_call | solution.py:430
  275.0 21.1 %dispatch.1 = (bf16[384,2048]{1,0:T(8,128)(2,1)}, bf16[4,1152,2048]{2,1,0:T(8,128)(2,1)}) custom-call(f32[16,16,384]{2,1,0:T(8,128)} %get-tuple-element.7.meta, bf16[16,384,2048]{2,1,0:T(8,128)(2,1)} %attend_gather.1.hf), custom_call_target="tpu_custom_call" | custom-call | tf_op jit(solution)/shard_map/dispatch/pallas_call | solution.py:522
